TPU v7x, 32 devices: a whole 2x2x4 slice. The times are simulated.
32 devices in a mesh: data: 2 (over x), pp: 4 (over z), ep: 4 (over y, core).
Axes of the slice: x: 2, y: 2, z: 4, core: 2. Of those that a mesh axis runs over, the one named last changes fastest.
Arguments:
- expert_out: bfloat16 [8, 1, 128, 32, 4096], P(('data', 'pp'), None, 'ep'), parts along dimension 0
- expert_id: int32 [8, 1, 256, 8], P(('data', 'pp'), None, 'ep'), parts along dimension 0
- slot_id: int32 [8, 1, 256, 8], P(('data', 'pp'), None, 'ep'), parts along dimension 0
- gate: float32 [8, 1, 256, 8], P(('data', 'pp'), None, 'ep'), parts along dimension 0
- resid: bfloat16 [8, 1, 256, 4096], P(('data', 'pp'), None, 'ep'), parts along dimension 0
- owner: int32 [8, 32], P(('data', 'pp')), parts along dimension 0
- norm_w: float32 [4, 4096], P('pp')
- w_q: bfloat16 [4, 4096, 8192], P('pp')
- w_k: bfloat16 [4, 4096, 8192], P('pp')
- w_v: bfloat16 [4, 4096, 8192], P('pp')
- w_o: bfloat16 [4, 8192, 4096], P('pp')
Outputs:
- output: bfloat16 [8, 1, 256, 4096], P(('data', 'pp'), None, 'ep'), parts along dimension 0
There are 2 independent parts. A program takes and returns all parts, laid end to end along the dimension named above; an argument that names none is the same for every part.
All inputs are finite; a program needn't handle non-finite values.
Results may differ from a plain program's by a relative error of at most 0.013572.
Values are sent between devices in bfloat16 or wider.
A program may use at most 1.25 GiB of HBM per device.

v0:
```python
import jax
import jax.numpy as jnp
from jax import lax
from jax.sharding import PartitionSpec as P

HEAD_DIM = 128
NORM_EPS = 1e-6


def attend_local(y_owned, norm_scale, w_q, w_k, w_v, w_o):
    n_micro, n_seqs, seq_len, model_dim = y_owned.shape
    n_heads = w_q.shape[1] // HEAD_DIM
    y_f32 = y_owned.astype(jnp.float32)
    inv_rms = lax.rsqrt(jnp.mean(y_f32 * y_f32, axis=-1, keepdims=True) + NORM_EPS)
    normed = (y_f32 * inv_rms * norm_scale).astype(jnp.bfloat16)

    def project(weight):
        proj_out = jnp.einsum('msld,de->msle', normed, weight, preferred_element_type=jnp.float32)
        return proj_out.astype(jnp.bfloat16).reshape(n_micro, n_seqs, seq_len, n_heads, HEAD_DIM)

    queries = project(w_q)
    key_vecs = project(w_k)
    values = project(w_v)
    scores = jnp.einsum('msqhe,mskhe->mshqk', queries, key_vecs, preferred_element_type=jnp.float32) * (HEAD_DIM ** -0.5)
    causal = jnp.arange(seq_len)[:, None] >= jnp.arange(seq_len)[None, :]
    attn_probs = jax.nn.softmax(jnp.where(causal, scores, -1e30), axis=-1).astype(jnp.bfloat16)
    head_mix = jnp.einsum('mshqk,mskhe->msqhe', attn_probs, values, preferred_element_type=jnp.float32).astype(jnp.bfloat16)
    out_proj = jnp.einsum('msqhe,hed->msqd', head_mix, w_o.reshape(n_heads, HEAD_DIM, model_dim), preferred_element_type=jnp.float32)
    return (y_f32 + out_proj.astype(jnp.bfloat16).astype(jnp.float32)).astype(jnp.bfloat16)


def combine_home(recv_out, expert_id, slot_id, gate, resid, dev_index, cap_dev):
    n_micro = recv_out.shape[0]
    model_dim = recv_out.shape[3]
    kept_mask = slot_id >= 0
    local_slot = jnp.where(kept_mask, slot_id - dev_index * cap_dev, 0)
    row_index = expert_id * cap_dev + local_slot
    flat_out = recv_out.reshape(n_micro, -1, model_dim)
    picked = jax.vmap(lambda out_table, row_ids: out_table[row_ids])(flat_out, row_index)
    weights = jnp.where(kept_mask, gate, 0.0)
    combined = jnp.sum(picked.astype(jnp.float32) * weights[..., None], axis=2)
    return (resid.astype(jnp.float32) + combined).astype(jnp.bfloat16)


def solution(mesh):
    n_stages = mesh.shape['pp']
    n_ep = mesh.shape['ep']
    next_rank = [(src_rank, (src_rank + 1) % n_stages) for src_rank in range(n_stages)]
    group_axes = ('data', 'pp')

    def device_step(expert_out, expert_id, slot_id, gate, resid, owner, norm_w, w_q, w_k, w_v, w_o):
        dev_index = lax.axis_index('ep')
        out_local = expert_out[0]
        cap_dev = out_local.shape[2] // n_ep
        recv_out = lax.all_to_all(out_local, 'ep', 2, 1, tiled=True)
        y_home = combine_home(recv_out, expert_id[0], slot_id[0], gate[0], resid[0], dev_index, cap_dev)
        y_next = lax.ppermute(y_home, 'pp', next_rank)
        n_micro, tok_dev, model_dim = y_next.shape
        seq_dev = owner.shape[1] // n_ep
        per_pair = seq_dev // n_ep
        owner_grid = owner[0].reshape(n_ep, seq_dev)
        src_dev = owner_grid // seq_dev
        positions = jnp.arange(seq_dev)
        send_rank = jnp.argsort(jnp.where(src_dev == dev_index, 0, seq_dev) + positions, axis=1)[:, :per_pair]
        send_seq = jnp.take_along_axis(owner_grid, send_rank, axis=1).reshape(seq_dev) - dev_index * seq_dev
        y_seqs = y_next.reshape(n_micro, seq_dev, tok_dev // seq_dev, model_dim)
        outgoing = jnp.take(y_seqs, send_seq, axis=1)
        incoming = lax.all_to_all(outgoing, 'ep', 1, 1, tiled=True)
        my_src = lax.dynamic_index_in_dim(src_dev, dev_index, 0, keepdims=False)
        arrival = jnp.argsort(my_src * seq_dev + positions)
        y_owned = jnp.take(incoming, jnp.argsort(arrival), axis=1)
        z_owned = attend_local(y_owned, norm_w[0], w_q[0], w_k[0], w_v[0], w_o[0])
        return z_owned.reshape(n_micro, tok_dev, model_dim)[None]

    tok_spec = P(group_axes, None, 'ep', None)
    weight_spec = P('pp', None, None)
    in_specs = (P(group_axes, None, 'ep', None, None), tok_spec, tok_spec, tok_spec, tok_spec, P(group_axes, None), P('pp', None), weight_spec, weight_spec, weight_spec, weight_spec)
    return jax.shard_map(device_step, mesh=mesh, in_specs=in_specs, out_specs=tok_spec, check_vma=False)
```

profile of v0, /device:TPU:0, one launch (start us, length us, event | category | flops | bytes accessed | tf_op | source)
XLA Modules:
  0.0 279.4 jit_solution(5384148336075202020)
XLA Ops:
  0.0 11.2 %copy.66 = bf16[1,1,32,32,4096]{4,2,3,1,0:T(8,128)(2,1)} copy(bf16[1,1,32,32,4096]{4,3,2,1,0:T(8,128)(2,1)} %param.13) | data formatting | bytes 16777216 | tf_op args[0]
  11.2 0.0 copy-start.2
  11.2 6.0 %all-to-all-start = ((bf16[1,32,32,4096]{3,1,0,2:T(8,128)(2,1)}), bf16[1,32,32,4096]{3,1,0,2:T(8,128)(2,1)}, u32[]{:S(2)}, u32[]{:S(2)}) async-start(bf16[1,32,32,4096]{3,1,0,2:T(8,128)(2,1)} %bitcast.129), calls=%async_computation | async-start | bytes 16777216 | tf_op jit(solution)/shard_map/all_to_all | solution.py:55
  17.2 0.0 copy-done.2
  17.2 0.0 copy-done.3
  17.2 0.1 copy.60
  17.3 0.1 reshape.268
  17.4 0.0 copy-done.4
  17.4 0.1 copy.61
  17.5 0.5 broadcast.261
  18.0 0.0 copy-done.5
  18.0 0.7 reduce.11
  18.7 0.1 reshape_squeeze.6
  18.8 0.1 copy.51
  18.9 0.7 sort.48
  19.6 0.1 copy.55
  19.7 0.1 reshape.274
  19.7 0.7 gather_fusion.1
  20.4 0.1 reshape.277
  20.5 0.1 copy.56
  20.6 0.1 copy.57
  20.7 0.1 sub.45
  20.8 0.2 multiply_reduce_fusion
  21.0 1.0 sort.49
  21.9 1.0 sort.50
  22.9 87.8 %all-to-all-done = bf16[1,32,32,4096]{3,1,0,2:T(8,128)(2,1)} async-done(((bf16[1,32,32,4096]{3,1,0,2:T(8,128)(2,1)}), bf16[1,32,32,4096]{3,1,0,2:T(8,128)(2,1)}, u32[]{:S(2)}, u32[]{:S(2)}) %all-to-all-start) | async-done | bytes 8388640 | tf_op jit(solution)/shard_map/all_to_all | solution.py:55
  110.7 11.3 %copy.59 = bf16[1,32,4,8,4096]{4,3,1,2,0:T(8,128)(2,1)} copy(bf16[1,32,4,8,4096]{4,1,3,2,0:T(8,128)(2,1)} %bitcast.3) | data formatting | bytes 16777216 | tf_op jit(solution)/shard_map/all_to_all | solution.py:55
  122.0 17.1 %gather_fusion = bf16[512,4096]{1,0:T(8,128)(2,1)} fusion(bf16[1,1024,4096]{2,1,0:T(8,128)(2,1)} %bitcast.128, s32[512]{0:T(512)S(1)} %reshape.268), kind=kCustom, calls=%fused_computation.2 | custom fusion | bytes 8392704 | tf_op jit(solution)/shard_map/vmap()/gather | solution.py:39
  139.1 5.7 %fusion.16 = f32[64,4096]{1,0:T(8,128)S(1)} fusion(bf16[512,4096]{1,0:T(8,128)(2,1)} %gather_fusion, f32[64,8]{1,0:T(8,128)S(1)} %copy.61), kind=kLoop, calls=%fused_computation.15 | loop fusion | flops 6029312 | bytes 5244928 | tf_op jit(solution)/shard_map/reduce_sum | solution.py:41
  144.8 0.0 copy-done.1
  144.8 0.1 fusion.38
  144.9 2.3 collective-permute-start
  147.2 14.6 %collective-permute-done = bf16[1,64,4096]{2,1,0:T(8,128)(2,1)S(1)} collective-permute-done((bf16[1,64,4096]{2,1,0:T(8,128)(2,1)S(1)}, bf16[1,64,4096]{2,1,0:T(8,128)(2,1)S(1)}, u32[]{:S(2)}, u32[]{:S(2)}) %collective-permute-start) | collective-permute-done | bytes 524320 | tf_op jit(solution)/shard_map/ppermute | solution.py:57
  161.8 0.6 gather_fusion.2
  162.4 0.9 bitcast_select_fusion.1
  163.3 3.7 %all-to-all-start.1 = ((bf16[1,8,8,4096]{3,2,0,1:T(8,128)(2,1)}), bf16[1,8,8,4096]{3,2,0,1:T(8,128)(2,1)S(1)}, u32[]{:S(2)}, u32[]{:S(2)}) async-start(bf16[1,8,8,4096]{3,2,0,1:T(8,128)(2,1)} %bitcast_select_fusion.1), calls=%async_computation.1 | async-start | bytes 1048576 | tf_op jit(solution)/shard_map/all_to_all | solution.py:68
  167.0 8.3 %all-to-all-done.1 = bf16[1,8,8,4096]{3,2,0,1:T(8,128)(2,1)S(1)} async-done(((bf16[1,8,8,4096]{3,2,0,1:T(8,128)(2,1)}), bf16[1,8,8,4096]{3,2,0,1:T(8,128)(2,1)S(1)}, u32[]{:S(2)}, u32[]{:S(2)}) %all-to-all-start.1) | async-done | bytes 524320 | tf_op jit(solution)/shard_map/all_to_all | solution.py:68
  175.3 0.6 gather_fusion.3
  175.9 0.3 fusion.35
  176.2 0.0 copy-done
  176.2 24.5 %fusion.30 = bf16[8,8,64,128]{3,1,2,0:T(8,128)(2,1)} fusion(bf16[1,4096,8192]{2,1,0:T(8,128)(2,1)} %param.22, f32[4096]{0:T(1024)S(1)} %bitcast.131, f32[8,8]{1,0:T(8,128)S(1)} %add_rsqrt_fusion, bf16[8,8,4096]{2,1,0:T(8,128)(2,1)S(1)} %gather_fusion.3, pred[8]{0:T(512)(128)(4,1)S(1)} %compare_and_fusion), kind=kOutput, calls=%fused_computation.30 | convolution fusion | flops 4296802304 | bytes 68698376 | tf_op jit(solution)/shard_map/msld,de->msle/dot_general | solution.py:18
  200.7 24.5 %fusion.27 = bf16[8,8,64,128]{3,1,2,0:T(8,128)(2,1)} fusion(bf16[1,4096,8192]{2,1,0:T(8,128)(2,1)} %param.20, f32[4096]{0:T(1024)S(1)} %bitcast.132, f32[8,8]{1,0:T(8,128)S(1)} %add_rsqrt_fusion, bf16[8,8,4096]{2,1,0:T(8,128)(2,1)S(1)} %gather_fusion.3, pred[8]{0:T(512)(128)(4,1)S(1)} %compare_and_fusion), kind=kOutput, calls=%fused_computation.29 | convolution fusion | flops 4296802304 | bytes 68698376 | tf_op jit(solution)/shard_map/msld,de->msle/dot_general | solution.py:18
  225.2 24.5 %fusion.24 = bf16[8,8,64,128]{3,1,2,0:T(8,128)(2,1)} fusion(bf16[1,4096,8192]{2,1,0:T(8,128)(2,1)} %param.21, f32[4096]{0:T(1024)S(1)} %bitcast.133, f32[8,8]{1,0:T(8,128)S(1)} %add_rsqrt_fusion, bf16[8,8,4096]{2,1,0:T(8,128)(2,1)S(1)} %gather_fusion.3, pred[8]{0:T(512)(128)(4,1)S(1)} %compare_and_fusion), kind=kOutput, calls=%fused_computation.28 | convolution fusion | flops 4296802304 | bytes 68698376 | tf_op jit(solution)/shard_map/msld,de->msle/dot_general | solution.py:18
  249.7 2.2 fusion.56
  251.9 0.6 copy.62
  252.5 0.9 fusion.55
  253.5 0.6 copy.63
  254.1 25.3 %fusion.22 = bf16[1,1,64,4096]{3,2,1,0:T(8,128)(2,1)} fusion(bf16[64,128,4096,1]{2,1,0,3:T(8,128)(2,1)} %bitcast.31, bf16[8,8,64,128]{3,1,2,0:T(8,128)(2,1)} %fusion.30, bf16[8,64,8,8]{3,2,1,0:T(8,128)(2,1)S(1)} %copy.63, bf16[8,8,4096]{2,1,0:T(8,128)(2,1)S(1)} %gather_fusion.3, pred[8]{0:T(512)(128)(4,1)S(1)} %compare_and_fusion), kind=kOutput, calls=%fused_computation.23 | convolution fusion | flops 4305453056 | bytes 69271560 | tf_op jit(solution)/shard_map/msqhe,hed->msqd/dot_general | solution.py:28
  (25 shorter events, 0.2 us)
Async XLA Ops:
  11.2 6.0 %copy-start.2 = (s32[1,1,64,8]{2,3,1,0:T(8,128)S(1)}, s32[1,1,64,8]{2,3,1,0:T(8,128)}, u32[]{:S(2)}) copy-start(s32[1,1,64,8]{2,3,1,0:T(8,128)} %param.15) | copy-start | bytes 6148
  11.2 6.0 %copy-start.3 = (s32[1,1,64,8]{2,3,1,0:T(8,128)S(1)}, s32[1,1,64,8]{2,3,1,0:T(8,128)}, u32[]{:S(2)}) copy-start(s32[1,1,64,8]{2,3,1,0:T(8,128)} %param.14) | copy-start | bytes 6148
  11.2 6.2 %copy-start.4 = (f32[1,1,64,8]{2,3,1,0:T(8,128)S(1)}, f32[1,1,64,8]{2,3,1,0:T(8,128)}, u32[]{:S(2)}) copy-start(f32[1,1,64,8]{2,3,1,0:T(8,128)} %param.16) | copy-start | bytes 6148
  11.2 6.8 %copy-start.5 = (s32[1,32]{1,0:T(1,128)S(1)}, s32[1,32]{1,0:T(1,128)}, u32[]{:S(2)}) copy-start(s32[1,32]{1,0:T(1,128)} %param.18) | copy-start | bytes 388
  11.2 99.5 %all-to-all-start = ((bf16[1,32,32,4096]{3,1,0,2:T(8,128)(2,1)}), bf16[1,32,32,4096]{3,1,0,2:T(8,128)(2,1)}, u32[]{:S(2)}, u32[]{:S(2)}) async-start(bf16[1,32,32,4096]{3,1,0,2:T(8,128)(2,1)} %bitcast.129), calls=%async_computation | async-start | bytes 16777216 | tf_op jit(solution)/shard_map/all_to_all | solution.py:55
  122.0 22.8 %copy-start.1 = (bf16[1,1,64,4096]{3,2,1,0:T(8,128)(2,1)S(1)}, bf16[1,1,64,4096]{3,2,1,0:T(8,128)(2,1)}, u32[]{:S(2)}) copy-start(bf16[1,1,64,4096]{3,2,1,0:T(8,128)(2,1)} %param.17) | copy-start | bytes 1572868
  139.1 37.1 %copy-start = (f32[1,4096]{1,0:T(1,128)S(1)}, f32[1,4096]{1,0:T(1,128)}, u32[]{:S(2)}) copy-start(f32[1,4096]{1,0:T(1,128)} %param.19) | copy-start | bytes 49156
  144.9 16.9 %collective-permute-start = (bf16[1,64,4096]{2,1,0:T(8,128)(2,1)S(1)}, bf16[1,64,4096]{2,1,0:T(8,128)(2,1)S(1)}, u32[]{:S(2)}, u32[]{:S(2)}) collective-permute-start(bf16[1,64,4096]{2,1,0:T(8,128)(2,1)S(1)} %fusion.38), channel_id=1, source_target_pairs={{0,4},{4,8},{8,12},{12,0},{1,5},{5,9},{9,13},{13,1},{2,6},{6,10},{... | collective-permute-start | bytes 1572872 | tf_op jit(solution)/shard_map/ppermute | solution.py:57
  163.3 12.0 %all-to-all-start.1 = ((bf16[1,8,8,4096]{3,2,0,1:T(8,128)(2,1)}), bf16[1,8,8,4096]{3,2,0,1:T(8,128)(2,1)S(1)}, u32[]{:S(2)}, u32[]{:S(2)}) async-start(bf16[1,8,8,4096]{3,2,0,1:T(8,128)(2,1)} %bitcast_select_fusion.1), calls=%async_computation.1 | async-start | bytes 1048576 | tf_op jit(solution)/shard_map/all_to_all | solution.py:68
where the time goes:
time: 280 us; the launch traced here: 279 us
  waiting for transfers between devices  111 us (40%)
  matrix products  101 us (36%)
  local copies, waits for them, and re-layouts  44.1 us (16%)
  starting transfers between devices  12 us (4%)
  other arithmetic  11.4 us (4%)
    all_to_all x1, waiting for transfers between devices, device_step(): recv_out = lax.all_to_all(out_local, 'ep', 2, 1, tiled=True)  87.8 us
    dot_general x3, matrix products, project(): jnp.einsum('msld,de->msle', normed, weight, preferred_element_type=jnp.fl...  73.5 us
    dot_general x1, matrix products, attend_local(): jnp.einsum('msqhe,hed->msqd', head_mix, w_o.reshape(n_heads, HEAD_DIM, mo...  25.3 us
    gather x4, local copies, waits for them, and re-layouts, combine_home(): out_table[row_ids]  17.3 us
    ppermute x1, waiting for transfers between devices, device_step(): y_next = lax.ppermute(y_home, 'pp', next_rank)  14.6 us
    unnamed x14, local copies, waits for them, and re-layouts  11.7 us
    all_to_all x1, local copies, waits for them, and re-layouts, device_step(): recv_out = lax.all_to_all(out_local, 'ep', 2, 1, tiled=True)  11.3 us
    all_to_all x1, waiting for transfers between devices, device_step(): incoming = lax.all_to_all(outgoing, 'ep', 1, 1, tiled=True)  8.31 us
  transfers between devices with their start and end apart: 3, of which 3 were waited for; matrix products, arithmetic and copies ran while one was open for 2% of the time, Pallas kernels for 0%

commit v1 on v0

v1 whole, which is shorter than its diff:
```python
import functools

import jax
import jax.numpy as jnp
from jax import lax
from jax.experimental import pallas as pl
from jax.experimental.pallas import tpu as pltpu
from jax.sharding import PartitionSpec as P

HEAD_DIM = 128
NORM_EPS = 1e-6
SEQ = 8
N_EP = 4
SLOTS = 24
RING_GROUPS = 4
ROWS = 32
PIECE = 16
LANES = 128
BF16_MAX = 3.3895314e38
MESH_ID = pl.DeviceIdType.MESH
F32 = jnp.float32
BF16 = jnp.bfloat16


def mm(a, b):
    return jnp.dot(a, b, preferred_element_type=F32)


def mm_t(a, b):
    return lax.dot_general(a, b, (((1,), (1,)), ((), ())), preferred_element_type=F32)


def split3(x):
    hi = jnp.clip(x, -BF16_MAX, BF16_MAX).astype(BF16)
    r1 = x - hi.astype(F32)
    mid = r1.astype(BF16)
    lo = (r1 - mid.astype(F32)).astype(BF16)
    return hi, mid, lo


def stage_kernel(
    n_pp, gw, exp_rows,
    meta_ref, own_ref, nw_ref, o_hbm, h_hbm, wq_hbm, wk_hbm, wv_hbm, wo_hbm,
    z_hbm,
    wbuf, pbuf, precv, yrecv, zsend, ybuf, xbuf, qkv, abuf, zbuf, hbuf, gbuf, metas, ownr, tok, mp,
    wsem, osem, hsem, msend, mrecv, osend, orecv, psend, prcv, ysend, yrcv, zsnd, zrcv, fsend, frcv, asend, arcv,
    outl, outs, outr,
):
    d_model = nw_ref.shape[1]
    half = d_model // 2
    e_half = wq_hbm.shape[1] // 2
    n_grp = e_half // gw
    slot_rows = wbuf.shape[1]
    n_out = half // gw
    grp_per_slot = slot_rows // gw
    tok_chip = 2 * 8 * SEQ
    tok_dev = 8 * SEQ
    n_chunk = tok_chip // ROWS
    n_piece = tok_chip // PIECE

    me = lax.axis_index("ep")
    core = lax.rem(me, 2)
    chip = me // 2
    partner = chip * 2 + (1 - core)
    across = (1 - chip) * 2 + core
    rank = lax.axis_index("pp")
    nxt = lax.rem(rank + 1, n_pp)
    prv = lax.rem(rank + n_pp - 1, n_pp)

    def remote(src, dst, s_sem, r_sem, dev):
        return pltpu.make_async_remote_copy(
            src_ref=src, dst_ref=dst, send_sem=s_sem, recv_sem=r_sem, device_id=dev, device_id_type=MESH_ID)

    def qkv_copy(mat, kh, g, slot):
        src = (wq_hbm, wk_hbm, wv_hbm)[mat]
        cols = pl.ds(pl.multiple_of(core * e_half + g * gw, gw), gw)
        return pltpu.make_async_copy(
            src.at[pl.ds(kh * slot_rows, slot_rows), cols], wbuf.at[slot], wsem.at[slot])

    def wo_copy(w):
        n, kq = w // 4, lax.rem(w, 4)
        rows = pl.ds(pl.multiple_of(kq * slot_rows, slot_rows), slot_rows)
        cols = pl.ds(pl.multiple_of(core * half + n * gw, gw), gw)
        slot = lax.rem(6 * n_grp + w, SLOTS)
        return pltpu.make_async_copy(wo_hbm.at[rows, cols], wbuf.at[slot], wsem.at[slot])

    o_slot = SLOTS - 4

    def o_copy(nb):
        return pltpu.make_async_copy(
            o_hbm.at[:, pl.ds(nb * gw, gw)],
            wbuf.at[o_slot + nb // 2, pl.ds((nb % 2) * exp_rows, exp_rows)], osem.at[nb])

    h_copy = pltpu.make_async_copy(h_hbm, hbuf, hsem)
    for nb in range(8):
        o_copy(nb).start()
    h_copy.start()
    first = [(g, j) for g in range(RING_GROUPS) for j in range(6)]
    for t, (g, j) in enumerate(first[:o_slot]):
        qkv_copy(j // 2, j % 2, g, t).start()

    barrier = pltpu.get_barrier_semaphore()
    for off in (1, 2, 3):
        pl.semaphore_signal(barrier, inc=1, device_id={"ep": lax.rem(me + off, N_EP)}, device_id_type=MESH_ID)
    pl.semaphore_signal(barrier, inc=1, device_id={"pp": nxt}, device_id_type=MESH_ID)
    pl.semaphore_signal(barrier, inc=1, device_id={"pp": prv}, device_id_type=MESH_ID)
    pl.semaphore_wait(barrier, 5)

    own_copy = remote(own_ref, ownr, osend, orecv, {"pp": prv})
    own_copy.start()
    meta_copies = [
        remote(meta_ref, metas.at[me], msend.at[off - 1], mrecv.at[off - 1], {"ep": lax.rem(me + off, N_EP)})
        for off in (1, 2, 3)]
    for cp in meta_copies:
        cp.start()
    metas[me] = meta_ref[...]
    own_copy.wait_recv()
    sub = lax.broadcasted_iota(jnp.int32, (SEQ, LANES), 0).astype(F32)
    for b in range(4 * SEQ):
        row = jnp.broadcast_to(ownr[b:b + 1, :], (SEQ, LANES))
        tok[b * SEQ:(b + 1) * SEQ, :] = row * float(SEQ) + sub
    for cp in meta_copies:
        cp.wait_recv()
    lane = lax.broadcasted_iota(jnp.int32, (4 * tok_dev, LANES), 1).astype(F32)
    routed = None
    for d in range(N_EP):
        hit = (tok[...] - float(d * tok_dev) == lane) & (lane < float(tok_dev))
        perm = jnp.where(hit, 1.0, 0.0).astype(BF16)
        parts = jnp.concatenate(split3(metas[d]), axis=0)
        term = mm_t(perm, parts)
        routed = term if routed is None else routed + term
    mp[:, 0:48] = routed

    for nb in range(8):
        o_copy(nb).wait()
    h_copy.wait()

    def pair_copy(s, row0):
        rows = pl.ds(row0, ROWS)
        return remote(pbuf.at[1 - core, rows], precv.at[rows], psend.at[s], prcv.at[s], {"ep": partner})

    def y_copy(k):
        src = pl.ds(pl.multiple_of((1 - chip) * tok_chip + k * PIECE, PIECE), PIECE)
        dst = pl.ds(pl.multiple_of(k * PIECE, PIECE), PIECE)
        return remote(pbuf.at[core, src], yrecv.at[dst], ysend.at[k], yrcv.at[k], {"ep": across})

    def chunk_row(s):
        blk = s // n_chunk
        base = ((1 - chip) * (1 - blk) + chip * blk) * tok_chip
        return pl.multiple_of(base + lax.rem(s, n_chunk) * ROWS, ROWS)

    def finish(s):
        row0 = chunk_row(s)
        rows = pl.ds(row0, ROWS)
        pair_copy(s, row0).wait_recv()
        pbuf[core, rows, :] = pbuf[core, rows, :] + precv[rows, :]

        @pl.when(s < n_chunk)
        def _():
            for p in range(ROWS // PIECE):
                y_copy(s * (ROWS // PIECE) + p).start()

    def chunk(s, carry):
        row0 = chunk_row(s)
        rows = pl.ds(row0, ROWS)
        here = mp[rows, :]
        shift = (me * exp_rows).astype(F32)
        target = here[:, 0:8] + here[:, 16:24] + here[:, 32:40] - shift
        for cb in range(exp_rows // 256):
            col = lax.broadcasted_iota(jnp.int32, (ROWS, 256), 1).astype(F32) + float(cb * 256)
            g0 = jnp.zeros((ROWS, 256), F32)
            g1 = jnp.zeros((ROWS, 256), F32)
            g2 = jnp.zeros((ROWS, 256), F32)
            for j in range(8):
                hit = col == target[:, j:j + 1]
                g0 = jnp.where(hit, here[:, 8 + j:9 + j], g0)
                g1 = jnp.where(hit, here[:, 24 + j:25 + j], g1)
                g2 = jnp.where(hit, here[:, 40 + j:41 + j], g2)
            cols = slice(cb * 256, (cb + 1) * 256)
            gbuf[0:ROWS, cols] = g0.astype(BF16)
            gbuf[ROWS:2 * ROWS, cols] = g1.astype(BF16)
            gbuf[2 * ROWS:3 * ROWS, cols] = g2.astype(BF16)
        lane_h = lax.broadcasted_iota(jnp.int32, (ROWS, LANES), 1).astype(F32)
        is_mine = (tok[rows, :] - (me * tok_dev).astype(F32) == lane_h) & (lane_h < float(tok_dev))
        pick = jnp.where(is_mine, 1.0, 0.0).astype(BF16)[:, :tok_dev]
        for side in range(2):
            hh = (1 - core) if side == 0 else core
            for q in range(4):
                o_cols = wbuf[o_slot + 2 * hh + q // 2, (q % 2) * exp_rows:(q % 2 + 1) * exp_rows, :]
                h_cols = hbuf[:, pl.ds(pl.multiple_of(hh * half + q * gw, gw), gw)]
                p3 = mm(gbuf[...], o_cols)
                total = p3[0:ROWS] + p3[ROWS:2 * ROWS] + p3[2 * ROWS:3 * ROWS] + mm(pick, h_cols)
                pbuf[hh, rows, q * gw:(q + 1) * gw] = total
            if side == 0:
                pair_copy(s, row0).start()

        @pl.when(s > 0)
        def _():
            finish(s - 1)
        return carry

    lax.fori_loop(0, 2 * n_chunk, chunk, 0)
    for t, (g, j) in list(enumerate(first))[o_slot:]:
        qkv_copy(j // 2, j % 2, g, t).start()
    finish(2 * n_chunk - 1)

    def z_copy(k):
        rows = pl.ds(k * PIECE, PIECE)
        return remote(zsend.at[rows], ybuf.at[core, rows], zsnd.at[k], zrcv.at[k], {"pp": nxt})

    def fwd_copy(k):
        rows = pl.ds(k * PIECE, PIECE)
        return remote(ybuf.at[core, rows], ybuf.at[core, rows], fsend.at[k], frcv.at[k], {"ep": partner})

    def norm(k):
        rows = slice(k * PIECE, (k + 1) * PIECE)
        lo = ybuf[0, rows, :].astype(F32)
        hi = ybuf[1, rows, :].astype(F32)
        sq = jnp.sum(lo * lo, axis=-1, keepdims=True) + jnp.sum(hi * hi, axis=-1, keepdims=True)
        inv = lax.rsqrt(sq / float(d_model) + NORM_EPS)
        xbuf[rows, 0:half] = (lo * inv * nw_ref[:, 0:half]).astype(BF16)
        xbuf[rows, half:d_model] = (hi * inv * nw_ref[:, half:d_model]).astype(BF16)

    for k in range(n_piece + 2):
        if k < n_piece:
            y_copy(k).wait_recv()
            near = pl.ds(pl.multiple_of(chip * tok_chip + k * PIECE, PIECE), PIECE)
            rows = slice(k * PIECE, (k + 1) * PIECE)
            zsend[rows, :] = (pbuf[core, near, :] + yrecv[rows, :]).astype(BF16)
            z_copy(k).start()
        if 1 <= k <= n_piece:
            z_copy(k - 1).wait_recv()
            fwd_copy(k - 1).start()
        if k >= 2:
            fwd_copy(k - 2).wait_recv()
            norm(k - 2)

    def a_copy(g):
        return remote(abuf.at[core * n_grp + g], abuf.at[core * n_grp + g], asend.at[g], arcv.at[g], {"ep": partner})

    r_id = lax.broadcasted_iota(jnp.int32, (tok_chip, tok_chip), 0)
    c_id = lax.broadcasted_iota(jnp.int32, (tok_chip, tok_chip), 1)
    mask = (r_id // SEQ == c_id // SEQ) & (c_id <= r_id)

    def group(g, carry):
        base = lax.rem(g, RING_GROUPS) * 6
        for j in range(6):
            qkv_copy(j // 2, j % 2, g, base + j).wait()
        for m in range(3):
            acc = mm(xbuf[:, 0:slot_rows], wbuf[base + 2 * m]) + mm(xbuf[:, slot_rows:2 * slot_rows], wbuf[base + 2 * m + 1])
            qkv[m] = acc.astype(BF16)

        @pl.when(g + RING_GROUPS < n_grp)
        def _():
            for j in range(6):
                qkv_copy(j // 2, j % 2, g + RING_GROUPS, base + j).start()

        for j in range(6):
            w = 6 * (g + RING_GROUPS - n_grp) + j

            @pl.when((w >= 0) & (w < 4 * n_out))
            def _():
                wo_copy(w).start()

        for hd in range(gw // HEAD_DIM):
            cols = slice(hd * HEAD_DIM, (hd + 1) * HEAD_DIM)
            s = mm_t(qkv[0, :, cols], qkv[1, :, cols]) * (HEAD_DIM ** -0.5)
            s = jnp.where(mask, s, -1e30)
            ex = jnp.exp(s - jnp.max(s, axis=-1, keepdims=True))
            prob = (ex / jnp.sum(ex, axis=-1, keepdims=True)).astype(BF16)
            abuf[core * n_grp + g, :, cols] = mm(prob, qkv[2, :, cols]).astype(BF16)
        a_copy(g).start()
        return carry

    lax.fori_loop(0, n_grp, group, 0)

    for g in range(n_grp):
        a_copy(g).wait_recv()

    def out_cols(n):
        return pl.ds(pl.multiple_of(core * half + n * gw, gw), gw)

    def out_local(n):
        rows = pl.ds(pl.multiple_of(core * tok_dev, tok_dev), tok_dev)
        return pltpu.make_async_copy(zbuf.at[n, rows], z_hbm.at[:, out_cols(n)], outl.at[n])

    def out_remote(n):
        rows = pl.ds(pl.multiple_of((1 - core) * tok_dev, tok_dev), tok_dev)
        return remote(zbuf.at[n, rows], z_hbm.at[:, out_cols(n)], outs.at[n], outr.at[n], {"ep": partner})

    def out_group(n, carry):
        for kq in range(4):
            wo_copy(4 * n + kq).wait()
        acc = None
        for kq in range(4):
            slot = lax.rem(6 * n_grp + 4 * n + kq, SLOTS)
            for gg in range(grp_per_slot):
                term = mm(abuf[kq * grp_per_slot + gg], wbuf[slot, gg * gw:(gg + 1) * gw, :])
                acc = term if acc is None else acc + term
        resid = ybuf[core, :, pl.ds(pl.multiple_of(n * gw, gw), gw)].astype(F32)
        zbuf[n] = (resid + acc.astype(BF16).astype(F32)).astype(BF16)
        out_local(n).start()
        out_remote(n).start()
        return carry

    lax.fori_loop(0, n_out, out_group, 0)

    own_copy.wait_send()
    for cp in meta_copies:
        cp.wait_send()
    for s in range(2 * n_chunk):
        pair_copy(s, chunk_row(s)).wait_send()
    for k in range(n_piece):
        y_copy(k).wait_send()
        z_copy(k).wait_send()
        fwd_copy(k).wait_send()
    for g in range(n_grp):
        a_copy(g).wait_send()
    for n in range(n_out):
        out_local(n).wait()
        out_remote(n).wait()


def solution(mesh):
    n_pp = mesh.shape['pp']
    group_axes = ('data', 'pp')

    def device_step(expert_out, expert_id, slot_id, gate, resid, owner, norm_w, w_q, w_k, w_v, w_o):
        d_model = resid.shape[3]
        tok_dev = resid.shape[2]
        n_exp, cap = expert_out.shape[2], expert_out.shape[3]
        exp_rows = n_exp * cap
        width = w_q.shape[2]
        gw = d_model // 8
        n_grp = width // 2 // gw
        n_out = d_model // 2 // gw
        tok_chip = 2 * tok_dev
        half = d_model // 2
        row_id = jnp.where(slot_id[0, 0] >= 0, expert_id[0, 0] * cap + slot_id[0, 0], -1).astype(F32)
        meta = jnp.concatenate([row_id.T, gate[0, 0].T], axis=0)
        meta = jnp.pad(meta, ((0, 0), (0, LANES - tok_dev)))
        own = jnp.broadcast_to(owner[0].astype(F32)[:, None], (owner.shape[1], LANES))
        vmem = pl.BlockSpec(memory_space=pltpu.VMEM)
        anym = pl.BlockSpec(memory_space=pl.ANY)
        dma = pltpu.SemaphoreType.DMA
        n_chunk2 = 2 * tok_chip // ROWS
        n_piece = tok_chip // PIECE
        out = pl.pallas_call(
            functools.partial(stage_kernel, n_pp, gw, exp_rows),
            out_shape=jax.ShapeDtypeStruct((tok_dev, d_model), BF16),
            in_specs=[vmem, vmem, vmem] + [anym] * 6,
            out_specs=anym,
            scratch_shapes=[
                pltpu.VMEM((SLOTS, d_model // 2, gw), BF16),
                pltpu.VMEM((2, 4 * tok_dev, half), F32),
                pltpu.VMEM((4 * tok_dev, half), F32),
                pltpu.VMEM((tok_chip, half), F32),
                pltpu.VMEM((tok_chip, half), BF16),
                pltpu.VMEM((2, tok_chip, half), BF16),
                pltpu.VMEM((tok_chip, d_model), BF16),
                pltpu.VMEM((3, tok_chip, gw), BF16),
                pltpu.VMEM((2 * n_grp, tok_chip, gw), BF16),
                pltpu.VMEM((n_out, tok_chip, gw), BF16),
                pltpu.VMEM((tok_dev, d_model), BF16),
                pltpu.VMEM((3 * ROWS, exp_rows), BF16),
                pltpu.VMEM((N_EP, 16, LANES), F32),
                pltpu.VMEM((4 * SEQ, LANES), F32),
                pltpu.VMEM((4 * tok_dev, LANES), F32),
                pltpu.VMEM((4 * tok_dev, LANES), F32),
                dma((SLOTS,)), dma((8,)), dma,
                dma((3,)), dma((3,)), dma, dma,
                dma((n_chunk2,)), dma((n_chunk2,)),
                dma((n_piece,)), dma((n_piece,)),
                dma((n_piece,)), dma((n_piece,)),
                dma((n_piece,)), dma((n_piece,)),
                dma((n_grp,)), dma((n_grp,)),
                dma((n_out,)), dma((n_out,)), dma((n_out,)),
            ],
            compiler_params=pltpu.CompilerParams(
                collective_id=0, has_side_effects=True, vmem_limit_bytes=67043328),
        )(meta, own, norm_w, expert_out.reshape(exp_rows, d_model), resid.reshape(tok_dev, d_model),
          w_q[0], w_k[0], w_v[0], w_o[0])
        return out.reshape(1, 1, tok_dev, d_model)

    tok_spec = P(group_axes, None, 'ep', None)
    weight_spec = P('pp', None, None)
    in_specs = (P(group_axes, None, 'ep', None, None), tok_spec, tok_spec, tok_spec, tok_spec, P(group_axes, None), P('pp', None), weight_spec, weight_spec, weight_spec, weight_spec)
    return jax.shard_map(device_step, mesh=mesh, in_specs=in_specs, out_specs=tok_spec, check_vma=False)
```

time: 280 us -> 90.1 us (0.32)
  waiting for transfers between devices: 111 us -> 0 us
  matrix products: 101 us -> 0 us
  Pallas kernels: 0 us -> 84.4 us
  local copies, waits for them, and re-layouts: 44.1 us -> 2.54 us
  starting transfers between devices: 12 us -> 0 us
  other arithmetic: 11.4 us -> 2.65 us
    dot_general x5 -> x0, matrix products: 101 us -> none  [the longest x3 73.5 us: project(): jnp.einsum('msld,de->msle', normed, weight, preferred_element_type=jnp.fl...]
    all_to_all x2 -> x0, waiting for transfers between devices: 96.1 us -> none  [the longest x1 87.8 us: device_step(): recv_out = lax.all_to_all(out_local, 'ep', 2, 1, tiled=True)]
    pallas_call x0 -> x1, Pallas kernels: none -> 84.4 us  [device_step(): pl.pallas_call(functools.partial(stage_kernel, n_pp, gw, exp_rows), out_s...]
    gather x11 -> x0, local copies, waits for them, and re-layouts: 19.5 us -> none  [the longest x4 17.3 us: combine_home(): out_table[row_ids]]
    ppermute x1 -> x0, waiting for transfers between devices: 14.6 us -> none  [device_step(): y_next = lax.ppermute(y_home, 'pp', next_rank)]
    all_to_all x1 -> x0, local copies, waits for them, and re-layouts: 11.3 us -> none  [device_step(): recv_out = lax.all_to_all(out_local, 'ep', 2, 1, tiled=True)]
    unnamed x14 -> x1, local copies, waits for them, and re-layouts: 11.7 us -> 1.87 us
    all_to_all x2 -> x0, starting transfers between devices: 9.67 us -> none  [the longest x1 5.98 us: device_step(): recv_out = lax.all_to_all(out_local, 'ep', 2, 1, tiled=True)]
  transfers between devices with their start and end apart: 3 -> 0, of which waited for: 3 -> 0; matrix products, arithmetic and copies ran while one was open for 2% -> 0% of each run, Pallas kernels for 0% -> 0%
where the time goes in v1:
time: 90.1 us; the launch traced here: 89.6 us
  Pallas kernels  84.4 us (94%)
  other arithmetic  2.65 us (3%)
  local copies, waits for them, and re-layouts  2.54 us (3%)
    pallas_call x1, Pallas kernels, device_step(): pl.pallas_call(functools.partial(stage_kernel, n_pp, gw, exp_rows), out_s...  84.4 us
    unnamed x1, local copies, waits for them, and re-layouts  1.87 us

profile of v1, /device:TPU:0, one launch (start us, length us, event | category | flops | bytes accessed | tf_op | source)
XLA Modules:
  0.0 89.6 jit_solution(1473015129061283229)
XLA Ops:
  0.0 0.7 convert_bitcast_fusion.1
  0.7 0.7 convert_bitcast_fusion
  1.4 1.3 %select_maximum_fusion.meta_ref = f32[16,128]{1,0:T(8,128)} fusion(f32[8,64]{1,0:T(8,128)} %bitcast.19, f32[8,64]{1,0:T(8,128)S(1)} %convert_bitcast_fusion), kind=kLoop, calls=%fused_computation | loop fusion | flops 8192 | bytes 12288 | tf_op jit(solution)/shard_map/concatenate | solution.py:340
  2.6 0.7 broadcast_in_dim.11.own_ref
  3.3 84.4 %shard_map.109 = bf16[64,4096]{1,0:T(8,128)(2,1)} custom-call(f32[16,128]{1,0:T(8,128)} %select_maximum_fusion.meta_ref, f32[32,128]{1,0:T(8,128)} %broadcast_in_dim.11.own_ref, f32[1,4096]{1,0:T(1,128)} %nw_ref.1, bf16[1024,4096]{1,0:T(8,128)(2,1)} %bitcast.16, bf16[64,4096]{1,0:T(8,128)(2,1)} %bitcast.18, bf16[4096,8192]{1,0:T(8,128)(2,1)} %bitcast.7.wq_hbm, ...), custom_call_target="tpu_custom_call" | custom-call | tf_op jit(solution)/shard_map/pallas_call | solution.py:348
  87.8 1.9 %copy.13 = bf16[1,1,64,4096]{3,2,1,0:T(8,128)(2,1)} copy(bf16[1,1,64,4096]{3,2,1,0:T(8,128)(2,1)} %bitcast.17) | data formatting | bytes 1048576

commit v2 on v1

--- a/solution.py
+++ b/solution.py
@@ -39,10 +39,10 @@
 
 
 def stage_kernel(
-    n_pp, gw, exp_rows,
-    meta_ref, own_ref, nw_ref, o_hbm, h_hbm, wq_hbm, wk_hbm, wv_hbm, wo_hbm,
+    n_pp, gw, exp_rows, cap,
+    eid_ref, slot_ref, gate_ref, own_ref, nw_ref, o_hbm, h_hbm, wq_hbm, wk_hbm, wv_hbm, wo_hbm,
     z_hbm,
-    wbuf, pbuf, precv, yrecv, zsend, ybuf, xbuf, qkv, abuf, zbuf, hbuf, gbuf, metas, ownr, tok, mp,
+    wbuf, pbuf, precv, yrecv, zsend, ybuf, xbuf, qkv, abuf, zbuf, hbuf, gbuf, metas, owns, ownr, tok, mp,
     wsem, osem, hsem, msend, mrecv, osend, orecv, psend, prcv, ysend, yrcv, zsnd, zrcv, fsend, frcv, asend, arcv,
     outl, outs, outr,
 ):
@@ -75,7 +75,7 @@
         src = (wq_hbm, wk_hbm, wv_hbm)[mat]
         cols = pl.ds(pl.multiple_of(core * e_half + g * gw, gw), gw)
         return pltpu.make_async_copy(
-            src.at[pl.ds(kh * slot_rows, slot_rows), cols], wbuf.at[slot], wsem.at[slot])
+            src.at[pl.ds(pl.multiple_of(kh * slot_rows, slot_rows), slot_rows), cols], wbuf.at[slot], wsem.at[slot])
 
     def wo_copy(w):
         n, kq = w // 4, lax.rem(w, 4)
@@ -95,25 +95,33 @@
     for nb in range(8):
         o_copy(nb).start()
     h_copy.start()
-    first = [(g, j) for g in range(RING_GROUPS) for j in range(6)]
-    for t, (g, j) in enumerate(first[:o_slot]):
-        qkv_copy(j // 2, j % 2, g, t).start()
 
     barrier = pltpu.get_barrier_semaphore()
     for off in (1, 2, 3):
         pl.semaphore_signal(barrier, inc=1, device_id={"ep": lax.rem(me + off, N_EP)}, device_id_type=MESH_ID)
     pl.semaphore_signal(barrier, inc=1, device_id={"pp": nxt}, device_id_type=MESH_ID)
     pl.semaphore_signal(barrier, inc=1, device_id={"pp": prv}, device_id_type=MESH_ID)
+
+    slot = slot_ref[...]
+    metas[me] = jnp.zeros((16, LANES), F32)
+    metas[me, 0:8, 0:tok_dev] = jnp.where(slot >= 0, eid_ref[...] * cap + slot, -1).astype(F32)
+    metas[me, 8:16, 0:tok_dev] = gate_ref[...]
+    n_seq = own_ref.shape[1]
+    diag = lax.broadcasted_iota(jnp.int32, (n_seq, n_seq), 0) == lax.broadcasted_iota(jnp.int32, (n_seq, n_seq), 1)
+    own_row = jnp.broadcast_to(own_ref[...].astype(F32), (n_seq, n_seq))
+    own_col = jnp.sum(jnp.where(diag, own_row, 0.0), axis=1, keepdims=True)
+    owns[...] = jnp.broadcast_to(own_col, (n_seq, LANES))
     pl.semaphore_wait(barrier, 5)
-
-    own_copy = remote(own_ref, ownr, osend, orecv, {"pp": prv})
+    own_copy = remote(owns, ownr, osend, orecv, {"pp": prv})
     own_copy.start()
     meta_copies = [
-        remote(meta_ref, metas.at[me], msend.at[off - 1], mrecv.at[off - 1], {"ep": lax.rem(me + off, N_EP)})
+        remote(metas.at[me], metas.at[me], msend.at[off - 1], mrecv.at[off - 1], {"ep": lax.rem(me + off, N_EP)})
         for off in (1, 2, 3)]
     for cp in meta_copies:
         cp.start()
-    metas[me] = meta_ref[...]
+    for step in range(2):
+        for m in range(3):
+            qkv_copy(m, step, 0, 2 * m + step).start()
     own_copy.wait_recv()
     sub = lax.broadcasted_iota(jnp.int32, (SEQ, LANES), 0).astype(F32)
     for b in range(4 * SEQ):
@@ -159,6 +167,18 @@
         def _():
             for p in range(ROWS // PIECE):
                 y_copy(s * (ROWS // PIECE) + p).start()
+
+    def prefetch(t):
+        g, kh = t // 2, lax.rem(t, 2)
+
+        @pl.when(t < 2 * RING_GROUPS)
+        def _():
+            qkv_copy(0, kh, g, 6 * g + kh).start()
+
+        @pl.when(t < 2 * RING_GROUPS - 2)
+        def _():
+            for m in range(1, 3):
+                qkv_copy(m, kh, g, 6 * g + 2 * m + kh).start()
 
     def chunk(s, carry):
         row0 = chunk_row(s)
@@ -193,16 +213,15 @@
                 pbuf[hh, rows, q * gw:(q + 1) * gw] = total
             if side == 0:
                 pair_copy(s, row0).start()
-
-        @pl.when(s > 0)
-        def _():
-            finish(s - 1)
+                prefetch(s + 2)
+
+        finish(s)
         return carry
 
     lax.fori_loop(0, 2 * n_chunk, chunk, 0)
-    for t, (g, j) in list(enumerate(first))[o_slot:]:
-        qkv_copy(j // 2, j % 2, g, t).start()
-    finish(2 * n_chunk - 1)
+    for kh in range(2):
+        for m in range(1, 3):
+            qkv_copy(m, kh, RING_GROUPS - 1, SLOTS - 6 + 2 * m + kh).start()
 
     def z_copy(k):
         rows = pl.ds(k * PIECE, PIECE)
@@ -336,19 +355,15 @@
         n_out = d_model // 2 // gw
         tok_chip = 2 * tok_dev
         half = d_model // 2
-        row_id = jnp.where(slot_id[0, 0] >= 0, expert_id[0, 0] * cap + slot_id[0, 0], -1).astype(F32)
-        meta = jnp.concatenate([row_id.T, gate[0, 0].T], axis=0)
-        meta = jnp.pad(meta, ((0, 0), (0, LANES - tok_dev)))
-        own = jnp.broadcast_to(owner[0].astype(F32)[:, None], (owner.shape[1], LANES))
         vmem = pl.BlockSpec(memory_space=pltpu.VMEM)
         anym = pl.BlockSpec(memory_space=pl.ANY)
         dma = pltpu.SemaphoreType.DMA
         n_chunk2 = 2 * tok_chip // ROWS
         n_piece = tok_chip // PIECE
         out = pl.pallas_call(
-            functools.partial(stage_kernel, n_pp, gw, exp_rows),
+            functools.partial(stage_kernel, n_pp, gw, exp_rows, cap),
             out_shape=jax.ShapeDtypeStruct((tok_dev, d_model), BF16),
-            in_specs=[vmem, vmem, vmem] + [anym] * 6,
+            in_specs=[vmem] * 5 + [anym] * 6,
             out_specs=anym,
             scratch_shapes=[
                 pltpu.VMEM((SLOTS, d_model // 2, gw), BF16),
@@ -365,6 +380,7 @@
                 pltpu.VMEM((3 * ROWS, exp_rows), BF16),
                 pltpu.VMEM((N_EP, 16, LANES), F32),
                 pltpu.VMEM((4 * SEQ, LANES), F32),
+                pltpu.VMEM((4 * SEQ, LANES), F32),
                 pltpu.VMEM((4 * tok_dev, LANES), F32),
                 pltpu.VMEM((4 * tok_dev, LANES), F32),
                 dma((SLOTS,)), dma((8,)), dma,
@@ -378,7 +394,7 @@
             ],
             compiler_params=pltpu.CompilerParams(
                 collective_id=0, has_side_effects=True, vmem_limit_bytes=67043328),
-        )(meta, own, norm_w, expert_out.reshape(exp_rows, d_model), resid.reshape(tok_dev, d_model),
+        )(expert_id[0, 0].T, slot_id[0, 0].T, gate[0, 0].T, owner, norm_w, expert_out.reshape(exp_rows, d_model), resid.reshape(tok_dev, d_model),
           w_q[0], w_k[0], w_v[0], w_o[0])
         return out.reshape(1, 1, tok_dev, d_model)
 

time: 90.1 us -> 81.4 us (0.903)
  Pallas kernels: 84.4 us -> 79.3 us
  other arithmetic: 2.65 us -> 0 us
    pallas_call x1, Pallas kernels: 84.4 us -> 79.3 us  [device_step(): pl.pallas_call(functools.partial(stage_kernel, n_pp, gw, exp_rows, cap),...]
    concatenate x1 -> x0, other arithmetic: 1.28 us -> none  [device_step(): meta = jnp.concatenate([row_id.T, gate[0, 0].T], axis=0)]
where the time goes in v2:
time: 81.4 us; the launch traced here: 81.1 us
  Pallas kernels  79.3 us (97%)
  local copies, waits for them, and re-layouts  1.87 us (2%)
    pallas_call x1, Pallas kernels, device_step(): pl.pallas_call(functools.partial(stage_kernel, n_pp, gw, exp_rows, cap),...  79.3 us
    unnamed x1, local copies, waits for them, and re-layouts  1.87 us

profile of v2, /device:TPU:0, one launch (start us, length us, event | category | flops | bytes accessed | tf_op | source)
XLA Modules:
  0.0 81.1 jit_solution(13379846312992766229)
XLA Ops:
  0.0 79.3 %shard_map.109 = bf16[64,4096]{1,0:T(8,128)(2,1)} custom-call(s32[8,64]{1,0:T(8,128)} %bitcast.19, s32[8,64]{1,0:T(8,128)} %bitcast.20, f32[8,64]{1,0:T(8,128)} %bitcast.21, s32[1,32]{1,0:T(1,128)} %own_ref.1, f32[1,4096]{1,0:T(1,128)} %nw_ref.1, bf16[1024,4096]{1,0:T(8,128)(2,1)} %bitcast.16, bf16[64,4096]{1,0:T(8,128)(2,1)} %bitcast.18, ...), custom_call_target="tpu_custom_call" | custom-call | tf_op jit(solution)/shard_map/pallas_call | solution.py:363
  79.3 1.9 %copy.13 = bf16[1,1,64,4096]{3,2,1,0:T(8,128)(2,1)} copy(bf16[1,1,64,4096]{3,2,1,0:T(8,128)(2,1)} %bitcast.17) | data formatting | bytes 1048576

commit v3 on v2

--- a/solution.py
+++ b/solution.py
@@ -42,7 +42,7 @@
     n_pp, gw, exp_rows, cap,
     eid_ref, slot_ref, gate_ref, own_ref, nw_ref, o_hbm, h_hbm, wq_hbm, wk_hbm, wv_hbm, wo_hbm,
     z_hbm,
-    wbuf, pbuf, precv, yrecv, zsend, ybuf, xbuf, qkv, abuf, zbuf, hbuf, gbuf, metas, owns, ownr, tok, mp,
+    wbuf, pbuf, precv, yrecv, zsend, ybuf, xbuf, qbuf, kbuf, vbuf, abuf, zbuf, hbuf, gbuf, metas, owns, ownr, tok, mp,
     wsem, osem, hsem, msend, mrecv, osend, orecv, psend, prcv, ysend, yrcv, zsnd, zrcv, fsend, frcv, asend, arcv,
     outl, outs, outr,
 ):
@@ -152,10 +152,15 @@
         dst = pl.ds(pl.multiple_of(k * PIECE, PIECE), PIECE)
         return remote(pbuf.at[core, src], yrecv.at[dst], ysend.at[k], yrcv.at[k], {"ep": across})
 
+    def chunk_of(s):
+        end = 2 * n_chunk - 1
+        far = lax.rem(s, 2) + (end - s) // end - s // end
+        return far, far * ((s + 1) // 2) + (1 - far) * ((s - 1) // 2)
+
     def chunk_row(s):
-        blk = s // n_chunk
-        base = ((1 - chip) * (1 - blk) + chip * blk) * tok_chip
-        return pl.multiple_of(base + lax.rem(s, n_chunk) * ROWS, ROWS)
+        far, idx = chunk_of(s)
+        base = ((1 - chip) * far + chip * (1 - far)) * tok_chip
+        return pl.multiple_of(base + idx * ROWS, ROWS)
 
     def finish(s):
         row0 = chunk_row(s)
@@ -163,10 +168,12 @@
         pair_copy(s, row0).wait_recv()
         pbuf[core, rows, :] = pbuf[core, rows, :] + precv[rows, :]
 
-        @pl.when(s < n_chunk)
+        far, idx = chunk_of(s)
+
+        @pl.when(far == 1)
         def _():
             for p in range(ROWS // PIECE):
-                y_copy(s * (ROWS // PIECE) + p).start()
+                y_copy(idx * (ROWS // PIECE) + p).start()
 
     def prefetch(t):
         g, kh = t // 2, lax.rem(t, 2)
@@ -179,6 +186,38 @@
         def _():
             for m in range(1, 3):
                 qkv_copy(m, kh, g, 6 * g + 2 * m + kh).start()
+
+    def piece(k):
+        return pl.ds(pl.multiple_of(k * PIECE, PIECE), PIECE)
+
+    def z_copy(k):
+        return remote(zsend.at[piece(k)], ybuf.at[core, piece(k)], zsnd.at[k], zrcv.at[k], {"pp": nxt})
+
+    def fwd_copy(k):
+        half_rows = ybuf.at[core, piece(k)]
+        return remote(half_rows, half_rows, fsend.at[k], frcv.at[k], {"ep": partner})
+
+    def step_y(k):
+        y_copy(k).wait_recv()
+        near = pl.ds(pl.multiple_of(chip * tok_chip + k * PIECE, PIECE), PIECE)
+        zsend[piece(k), :] = (pbuf[core, near, :] + yrecv[piece(k), :]).astype(BF16)
+        z_copy(k).start()
+
+    def step_z(k):
+        z_copy(k).wait_recv()
+        fwd_copy(k).start()
+
+    def step_norm(k):
+        fwd_copy(k).wait_recv()
+        rows = piece(k)
+        lo = ybuf[0, rows, :].astype(F32)
+        hi = ybuf[1, rows, :].astype(F32)
+        sq = jnp.sum(lo * lo, axis=-1, keepdims=True) + jnp.sum(hi * hi, axis=-1, keepdims=True)
+        inv = lax.rsqrt(sq / float(d_model) + NORM_EPS)
+        xbuf[rows, 0:half] = (lo * inv * nw_ref[:, 0:half]).astype(BF16)
+        xbuf[rows, half:d_model] = (hi * inv * nw_ref[:, half:d_model]).astype(BF16)
+
+    z_lag, f_lag, first_z = 2, 4, 2
 
     def chunk(s, carry):
         row0 = chunk_row(s)
@@ -216,43 +255,23 @@
                 prefetch(s + 2)
 
         finish(s)
+        for lag, step in ((first_z, step_y), (first_z + z_lag, step_z), (first_z + f_lag, step_norm)):
+            @pl.when(s >= lag)
+            def _():
+                step(s - lag)
         return carry
 
     lax.fori_loop(0, 2 * n_chunk, chunk, 0)
     for kh in range(2):
         for m in range(1, 3):
             qkv_copy(m, kh, RING_GROUPS - 1, SLOTS - 6 + 2 * m + kh).start()
-
-    def z_copy(k):
-        rows = pl.ds(k * PIECE, PIECE)
-        return remote(zsend.at[rows], ybuf.at[core, rows], zsnd.at[k], zrcv.at[k], {"pp": nxt})
-
-    def fwd_copy(k):
-        rows = pl.ds(k * PIECE, PIECE)
-        return remote(ybuf.at[core, rows], ybuf.at[core, rows], fsend.at[k], frcv.at[k], {"ep": partner})
-
-    def norm(k):
-        rows = slice(k * PIECE, (k + 1) * PIECE)
-        lo = ybuf[0, rows, :].astype(F32)
-        hi = ybuf[1, rows, :].astype(F32)
-        sq = jnp.sum(lo * lo, axis=-1, keepdims=True) + jnp.sum(hi * hi, axis=-1, keepdims=True)
-        inv = lax.rsqrt(sq / float(d_model) + NORM_EPS)
-        xbuf[rows, 0:half] = (lo * inv * nw_ref[:, 0:half]).astype(BF16)
-        xbuf[rows, half:d_model] = (hi * inv * nw_ref[:, half:d_model]).astype(BF16)
-
-    for k in range(n_piece + 2):
+    for k in range(2 * n_chunk - first_z, n_piece + f_lag):
         if k < n_piece:
-            y_copy(k).wait_recv()
-            near = pl.ds(pl.multiple_of(chip * tok_chip + k * PIECE, PIECE), PIECE)
-            rows = slice(k * PIECE, (k + 1) * PIECE)
-            zsend[rows, :] = (pbuf[core, near, :] + yrecv[rows, :]).astype(BF16)
-            z_copy(k).start()
-        if 1 <= k <= n_piece:
-            z_copy(k - 1).wait_recv()
-            fwd_copy(k - 1).start()
-        if k >= 2:
-            fwd_copy(k - 2).wait_recv()
-            norm(k - 2)
+            step_y(k)
+        if z_lag <= k < n_piece + z_lag:
+            step_z(k - z_lag)
+        if k >= f_lag:
+            step_norm(k - f_lag)
 
     def a_copy(g):
         return remote(abuf.at[core * n_grp + g], abuf.at[core * n_grp + g], asend.at[g], arcv.at[g], {"ep": partner})
@@ -261,14 +280,25 @@
     c_id = lax.broadcasted_iota(jnp.int32, (tok_chip, tok_chip), 1)
     mask = (r_id // SEQ == c_id // SEQ) & (c_id <= r_id)
 
-    def group(g, carry):
-        base = lax.rem(g, RING_GROUPS) * 6
-        for j in range(6):
-            qkv_copy(j // 2, j % 2, g, base + j).wait()
-        for m in range(3):
-            acc = mm(xbuf[:, 0:slot_rows], wbuf[base + 2 * m]) + mm(xbuf[:, slot_rows:2 * slot_rows], wbuf[base + 2 * m + 1])
-            qkv[m] = acc.astype(BF16)
-
+    n_head = gw // HEAD_DIM
+    head = [slice(hd * HEAD_DIM, (hd + 1) * HEAD_DIM) for hd in range(n_head)]
+
+    def project(m, base):
+        acc = mm(xbuf[:, 0:slot_rows], wbuf[base + 2 * m]) + mm(xbuf[:, slot_rows:2 * slot_rows], wbuf[base + 2 * m + 1])
+        return acc.astype(BF16)
+
+    def scores(hd):
+        return mm_t(qbuf[:, head[hd]], kbuf[:, head[hd]]) * (HEAD_DIM ** -0.5)
+
+    def softmax(s):
+        s = jnp.where(mask, s, -1e30)
+        ex = jnp.exp(s - jnp.max(s, axis=-1, keepdims=True))
+        return (ex / jnp.sum(ex, axis=-1, keepdims=True)).astype(BF16)
+
+    def mix(g, hd, prob):
+        abuf[core * n_grp + g, :, head[hd]] = mm(prob, vbuf[:, head[hd]]).astype(BF16)
+
+    def refill(g, base):
         @pl.when(g + RING_GROUPS < n_grp)
         def _():
             for j in range(6):
@@ -281,17 +311,38 @@
             def _():
                 wo_copy(w).start()
 
-        for hd in range(gw // HEAD_DIM):
-            cols = slice(hd * HEAD_DIM, (hd + 1) * HEAD_DIM)
-            s = mm_t(qkv[0, :, cols], qkv[1, :, cols]) * (HEAD_DIM ** -0.5)
-            s = jnp.where(mask, s, -1e30)
-            ex = jnp.exp(s - jnp.max(s, axis=-1, keepdims=True))
-            prob = (ex / jnp.sum(ex, axis=-1, keepdims=True)).astype(BF16)
-            abuf[core * n_grp + g, :, cols] = mm(prob, qkv[2, :, cols]).astype(BF16)
-        a_copy(g).start()
+    def wait_group(g, base):
+        for j in range(6):
+            qkv_copy(j // 2, j % 2, g, base + j).wait()
+
+    wait_group(0, 0)
+    qbuf[...] = project(0, 0)
+    kbuf[...] = project(1, 0)
+    vbuf[...] = project(2, 0)
+    refill(0, 0)
+
+    def group(g, carry):
+        base = lax.rem(g, RING_GROUPS) * 6
+        wait_group(g, base)
+        raw = [scores(hd) for hd in range(n_head)]
+        q_new = project(0, base)
+        probs = [softmax(raw[hd]) for hd in range(n_head)]
+        qbuf[...] = q_new
+        k_new = project(1, base)
+        kbuf[...] = k_new
+        for hd in range(n_head):
+            mix(g - 1, hd, probs[hd])
+        v_new = project(2, base)
+        vbuf[...] = v_new
+        a_copy(g - 1).start()
+        refill(g, base)
         return carry
 
-    lax.fori_loop(0, n_grp, group, 0)
+    lax.fori_loop(1, n_grp, group, 0)
+    last = n_grp - 1
+    for hd, prob in enumerate([softmax(scores(hd)) for hd in range(n_head)]):
+        mix(last, hd, prob)
+    a_copy(last).start()
 
     for g in range(n_grp):
         a_copy(g).wait_recv()
@@ -373,7 +424,9 @@
                 pltpu.VMEM((tok_chip, half), BF16),
                 pltpu.VMEM((2, tok_chip, half), BF16),
                 pltpu.VMEM((tok_chip, d_model), BF16),
-                pltpu.VMEM((3, tok_chip, gw), BF16),
+                pltpu.VMEM((tok_chip, gw), BF16),
+                pltpu.VMEM((tok_chip, gw), BF16),
+                pltpu.VMEM((tok_chip, gw), BF16),
                 pltpu.VMEM((2 * n_grp, tok_chip, gw), BF16),
                 pltpu.VMEM((n_out, tok_chip, gw), BF16),
                 pltpu.VMEM((tok_dev, d_model), BF16),

time: 81.4 us -> 76 us (0.934)
  Pallas kernels: 79.3 us -> 73.8 us
    pallas_call x1, Pallas kernels: 79.3 us -> 73.8 us  [device_step(): pl.pallas_call(functools.partial(stage_kernel, n_pp, gw, exp_rows, cap),...]
where the time goes in v3:
time: 76 us; the launch traced here: 75.7 us
  Pallas kernels  73.8 us (97%)
  local copies, waits for them, and re-layouts  1.87 us (2%)
    pallas_call x1, Pallas kernels, device_step(): pl.pallas_call(functools.partial(stage_kernel, n_pp, gw, exp_rows, cap),...  73.8 us
    unnamed x1, local copies, waits for them, and re-layouts  1.87 us

profile of v3, /device:TPU:0, one launch (start us, length us, event | category | flops | bytes accessed | tf_op | source)
XLA Modules:
  0.0 75.7 jit_solution(13622396772604600654)
XLA Ops:
  0.0 73.8 %shard_map.109 = bf16[64,4096]{1,0:T(8,128)(2,1)} custom-call(s32[8,64]{1,0:T(8,128)} %bitcast.19, s32[8,64]{1,0:T(8,128)} %bitcast.20, f32[8,64]{1,0:T(8,128)} %bitcast.21, s32[1,32]{1,0:T(1,128)} %own_ref.1, f32[1,4096]{1,0:T(1,128)} %nw_ref.1, bf16[1024,4096]{1,0:T(8,128)(2,1)} %bitcast.16, bf16[64,4096]{1,0:T(8,128)(2,1)} %bitcast.18, ...), custom_call_target="tpu_custom_call" | custom-call | tf_op jit(solution)/shard_map/pallas_call | solution.py:414
  73.8 1.9 %copy.13 = bf16[1,1,64,4096]{3,2,1,0:T(8,128)(2,1)} copy(bf16[1,1,64,4096]{3,2,1,0:T(8,128)(2,1)} %bitcast.17) | data formatting | bytes 1048576

commit v4 on v3

--- a/solution.py
+++ b/solution.py
@@ -11,7 +11,7 @@
 NORM_EPS = 1e-6
 SEQ = 8
 N_EP = 4
-SLOTS = 24
+SLOTS = 27
 RING_GROUPS = 4
 ROWS = 32
 PIECE = 16
@@ -40,13 +40,14 @@
 
 def stage_kernel(
     n_pp, gw, exp_rows, cap,
-    eid_ref, slot_ref, gate_ref, own_ref, nw_ref, o_hbm, h_hbm, wq_hbm, wk_hbm, wv_hbm, wo_hbm,
-    z_hbm,
-    wbuf, pbuf, precv, yrecv, zsend, ybuf, xbuf, qbuf, kbuf, vbuf, abuf, zbuf, hbuf, gbuf, metas, owns, ownr, tok, mp,
+    eid_hbm, slot_hbm, gate_hbm, own_hbm, nw_hbm, o_hbm, h_hbm, wq_hbm, wk_hbm, wv_hbm, wo_hbm,
+    z_hbm, y_hbm,
+    eid_ref, slot_ref, gate_ref, own_ref, nw_ref, insem, youtsem,
+    wbuf, pkeep, pout, precv, yrecv, ybuf, xbuf, qbuf, kbuf, vbuf, abuf, gbuf, metas, owns, ownr, tok, mp,
     wsem, osem, hsem, msend, mrecv, osend, orecv, psend, prcv, ysend, yrcv, zsnd, zrcv, fsend, frcv, asend, arcv,
     outl, outs, outr,
 ):
-    d_model = nw_ref.shape[1]
+    d_model = nw_hbm.shape[1]
     half = d_model // 2
     e_half = wq_hbm.shape[1] // 2
     n_grp = e_half // gw
@@ -91,16 +92,27 @@
             o_hbm.at[:, pl.ds(nb * gw, gw)],
             wbuf.at[o_slot + nb // 2, pl.ds((nb % 2) * exp_rows, exp_rows)], osem.at[nb])
 
-    h_copy = pltpu.make_async_copy(h_hbm, hbuf, hsem)
-    for nb in range(8):
-        o_copy(nb).start()
-    h_copy.start()
+    def h_copy(nb):
+        return pltpu.make_async_copy(
+            h_hbm.at[:, pl.ds(nb * gw, gw)], abuf.at[(1 - core) * n_grp + nb, pl.ds(0, tok_dev)], hsem.at[nb])
 
     barrier = pltpu.get_barrier_semaphore()
     for off in (1, 2, 3):
         pl.semaphore_signal(barrier, inc=1, device_id={"ep": lax.rem(me + off, N_EP)}, device_id_type=MESH_ID)
     pl.semaphore_signal(barrier, inc=1, device_id={"pp": nxt}, device_id_type=MESH_ID)
     pl.semaphore_signal(barrier, inc=1, device_id={"pp": prv}, device_id_type=MESH_ID)
+    in_copies = [
+        pltpu.make_async_copy(src, dst, insem.at[n]) for n, (src, dst) in enumerate((
+            (eid_hbm, eid_ref), (slot_hbm, slot_ref), (gate_hbm, gate_ref), (own_hbm, own_ref), (nw_hbm, nw_ref)))]
+    for cp in in_copies:
+        cp.start()
+    for nb in range(8):
+        o_copy(nb).start()
+    for nb in range(8):
+        h_copy(nb).start()
+    for cp in in_copies:
+        cp.wait()
+
 
     slot = slot_ref[...]
     metas[me] = jnp.zeros((16, LANES), F32)
@@ -141,16 +153,16 @@
 
     for nb in range(8):
         o_copy(nb).wait()
-    h_copy.wait()
-
-    def pair_copy(s, row0):
-        rows = pl.ds(row0, ROWS)
-        return remote(pbuf.at[1 - core, rows], precv.at[rows], psend.at[s], prcv.at[s], {"ep": partner})
-
-    def y_copy(k):
-        src = pl.ds(pl.multiple_of((1 - chip) * tok_chip + k * PIECE, PIECE), PIECE)
-        dst = pl.ds(pl.multiple_of(k * PIECE, PIECE), PIECE)
-        return remote(pbuf.at[core, src], yrecv.at[dst], ysend.at[k], yrcv.at[k], {"ep": across})
+        h_copy(nb).wait()
+
+    def pair_copy(s):
+        slot = lax.rem(s, 2)
+        return remote(pout.at[slot], precv.at[slot], psend.at[s], prcv.at[s], {"ep": partner})
+
+    def y_copy(k, n):
+        src = pl.ds(pl.multiple_of((1 - chip) * tok_chip + k * PIECE, PIECE), n * PIECE)
+        dst = pl.ds(pl.multiple_of(k * PIECE, PIECE), n * PIECE)
+        return remote(pkeep.at[src], yrecv.at[dst], ysend.at[k], yrcv.at[k], {"ep": across})
 
     def chunk_of(s):
         end = 2 * n_chunk - 1
@@ -165,15 +177,19 @@
     def finish(s):
         row0 = chunk_row(s)
         rows = pl.ds(row0, ROWS)
-        pair_copy(s, row0).wait_recv()
-        pbuf[core, rows, :] = pbuf[core, rows, :] + precv[rows, :]
+        pair_copy(s).wait_recv()
+        pkeep[rows, :] = pkeep[rows, :] + precv[lax.rem(s, 2)]
 
         far, idx = chunk_of(s)
 
-        @pl.when(far == 1)
-        def _():
-            for p in range(ROWS // PIECE):
-                y_copy(idx * (ROWS // PIECE) + p).start()
+        @pl.when(far * (n_chunk - 1 - idx) > 0)
+        def _():
+            y_copy(2 * idx, 2).start()
+
+        @pl.when(far * (idx // (n_chunk - 1)) > 0)
+        def _():
+            y_copy(n_piece - 2, 1).start()
+            y_copy(n_piece - 1, 1).start()
 
     def prefetch(t):
         g, kh = t // 2, lax.rem(t, 2)
@@ -181,26 +197,35 @@
         @pl.when(t < 2 * RING_GROUPS)
         def _():
             qkv_copy(0, kh, g, 6 * g + kh).start()
-
-        @pl.when(t < 2 * RING_GROUPS - 2)
-        def _():
-            for m in range(1, 3):
-                qkv_copy(m, kh, g, 6 * g + 2 * m + kh).start()
+            qkv_copy(1, kh, g, 6 * g + 2 + kh).start()
+
+        @pl.when(t < 2 * RING_GROUPS - 1)
+        def _():
+            qkv_copy(2, kh, g, 6 * g + 4 + kh).start()
 
     def piece(k):
         return pl.ds(pl.multiple_of(k * PIECE, PIECE), PIECE)
 
     def z_copy(k):
-        return remote(zsend.at[piece(k)], ybuf.at[core, piece(k)], zsnd.at[k], zrcv.at[k], {"pp": nxt})
+        return remote(
+            abuf.at[pl.ds(core * n_grp, n_out), piece(k)], ybuf.at[pl.ds(core * n_out, n_out), piece(k)],
+            zsnd.at[k], zrcv.at[k], {"pp": nxt})
 
     def fwd_copy(k):
-        half_rows = ybuf.at[core, piece(k)]
+        half_rows = ybuf.at[pl.ds(core * n_out, n_out), piece(k)]
         return remote(half_rows, half_rows, fsend.at[k], frcv.at[k], {"ep": partner})
 
     def step_y(k):
-        y_copy(k).wait_recv()
+        if isinstance(k, int) and k >= n_piece - 2:
+            y_copy(k, 1).wait_recv()
+        else:
+            @pl.when(lax.rem(k, 2) == 0)
+            def _():
+                y_copy(k, 2).wait_recv()
         near = pl.ds(pl.multiple_of(chip * tok_chip + k * PIECE, PIECE), PIECE)
-        zsend[piece(k), :] = (pbuf[core, near, :] + yrecv[piece(k), :]).astype(BF16)
+        for b in range(n_out):
+            cols = slice(b * gw, (b + 1) * gw)
+            abuf[core * n_grp + b, piece(k), :] = (pkeep[near, cols] + yrecv[piece(k), cols]).astype(BF16)
         z_copy(k).start()
 
     def step_z(k):
@@ -210,14 +235,17 @@
     def step_norm(k):
         fwd_copy(k).wait_recv()
         rows = piece(k)
-        lo = ybuf[0, rows, :].astype(F32)
-        hi = ybuf[1, rows, :].astype(F32)
-        sq = jnp.sum(lo * lo, axis=-1, keepdims=True) + jnp.sum(hi * hi, axis=-1, keepdims=True)
+        sq = None
+        for b in range(2 * n_out):
+            val = ybuf[b, rows, :].astype(F32)
+            term = jnp.sum(val * val, axis=-1, keepdims=True)
+            sq = term if sq is None else sq + term
         inv = lax.rsqrt(sq / float(d_model) + NORM_EPS)
-        xbuf[rows, 0:half] = (lo * inv * nw_ref[:, 0:half]).astype(BF16)
-        xbuf[rows, half:d_model] = (hi * inv * nw_ref[:, half:d_model]).astype(BF16)
-
-    z_lag, f_lag, first_z = 2, 4, 2
+        for b in range(2 * n_out):
+            cols = slice(b * gw, (b + 1) * gw)
+            xbuf[rows, cols] = (ybuf[b, rows, :].astype(F32) * inv * nw_ref[:, cols]).astype(BF16)
+
+    z_lag, f_lag, first_z = 4, 6, 2
 
     def chunk(s, carry):
         row0 = chunk_row(s)
@@ -242,16 +270,23 @@
         lane_h = lax.broadcasted_iota(jnp.int32, (ROWS, LANES), 1).astype(F32)
         is_mine = (tok[rows, :] - (me * tok_dev).astype(F32) == lane_h) & (lane_h < float(tok_dev))
         pick = jnp.where(is_mine, 1.0, 0.0).astype(BF16)[:, :tok_dev]
+        @pl.when(s >= 2)
+        def _():
+            pair_copy(s - 2).wait_send()
+
         for side in range(2):
             hh = (1 - core) if side == 0 else core
             for q in range(4):
                 o_cols = wbuf[o_slot + 2 * hh + q // 2, (q % 2) * exp_rows:(q % 2 + 1) * exp_rows, :]
-                h_cols = hbuf[:, pl.ds(pl.multiple_of(hh * half + q * gw, gw), gw)]
+                h_cols = abuf[(1 - core) * n_grp + hh * n_out + q, 0:tok_dev, :]
                 p3 = mm(gbuf[...], o_cols)
                 total = p3[0:ROWS] + p3[ROWS:2 * ROWS] + p3[2 * ROWS:3 * ROWS] + mm(pick, h_cols)
-                pbuf[hh, rows, q * gw:(q + 1) * gw] = total
+                if side == 0:
+                    pout[lax.rem(s, 2), :, q * gw:(q + 1) * gw] = total
+                else:
+                    pkeep[rows, q * gw:(q + 1) * gw] = total
             if side == 0:
-                pair_copy(s, row0).start()
+                pair_copy(s).start()
                 prefetch(s + 2)
 
         finish(s)
@@ -262,9 +297,8 @@
         return carry
 
     lax.fori_loop(0, 2 * n_chunk, chunk, 0)
-    for kh in range(2):
-        for m in range(1, 3):
-            qkv_copy(m, kh, RING_GROUPS - 1, SLOTS - 6 + 2 * m + kh).start()
+    for t in range(o_slot, SLOTS):
+        qkv_copy(t % 6 // 2, t % 2, t // 6, t).start()
     for k in range(2 * n_chunk - first_z, n_piece + f_lag):
         if k < n_piece:
             step_y(k)
@@ -283,8 +317,11 @@
     n_head = gw // HEAD_DIM
     head = [slice(hd * HEAD_DIM, (hd + 1) * HEAD_DIM) for hd in range(n_head)]
 
-    def project(m, base):
-        acc = mm(xbuf[:, 0:slot_rows], wbuf[base + 2 * m]) + mm(xbuf[:, slot_rows:2 * slot_rows], wbuf[base + 2 * m + 1])
+    def slot_of(g, j):
+        return lax.rem(6 * g + j, SLOTS)
+
+    def project(m, g):
+        acc = mm(xbuf[:, 0:slot_rows], wbuf[slot_of(g, 2 * m)]) + mm(xbuf[:, slot_rows:2 * slot_rows], wbuf[slot_of(g, 2 * m + 1)])
         return acc.astype(BF16)
 
     def scores(hd):
@@ -298,44 +335,53 @@
     def mix(g, hd, prob):
         abuf[core * n_grp + g, :, head[hd]] = mm(prob, vbuf[:, head[hd]]).astype(BF16)
 
-    def refill(g, base):
-        @pl.when(g + RING_GROUPS < n_grp)
-        def _():
-            for j in range(6):
-                qkv_copy(j // 2, j % 2, g + RING_GROUPS, base + j).start()
-
+    def refill(g, j):
+        ahead = j + SLOTS
+        g2, j2 = g + ahead // 6, ahead % 6
+
+        @pl.when(g2 < n_grp)
+        def _():
+            qkv_copy(j2 // 2, j2 % 2, g2, slot_of(g, j)).start()
+
+        w = 6 * (g2 - n_grp) + j2
+
+        @pl.when((w >= 0) & (w < 4 * n_out))
+        def _():
+            wo_copy(w).start()
+
+    def wait_group(g):
         for j in range(6):
-            w = 6 * (g + RING_GROUPS - n_grp) + j
-
-            @pl.when((w >= 0) & (w < 4 * n_out))
-            def _():
-                wo_copy(w).start()
-
-    def wait_group(g, base):
-        for j in range(6):
-            qkv_copy(j // 2, j % 2, g, base + j).wait()
-
-    wait_group(0, 0)
-    qbuf[...] = project(0, 0)
-    kbuf[...] = project(1, 0)
-    vbuf[...] = project(2, 0)
-    refill(0, 0)
+            qkv_copy(j // 2, j % 2, g, slot_of(g, j)).wait()
+
+    def y_out(b):
+        rows = pl.ds(pl.multiple_of(core * tok_dev, tok_dev), tok_dev)
+        return pltpu.make_async_copy(ybuf.at[b, rows], y_hbm.at[:, pl.ds(b * gw, gw)], youtsem.at[b])
+
+    for b in range(2 * n_out):
+        y_out(b).start()
+    for k in range(n_piece):
+        z_copy(k).wait_send()
+    wait_group(0)
+    for m, buf in enumerate((qbuf, kbuf, vbuf)):
+        buf[...] = project(m, 0)
+        refill(0, 2 * m)
+        refill(0, 2 * m + 1)
 
     def group(g, carry):
-        base = lax.rem(g, RING_GROUPS) * 6
-        wait_group(g, base)
+        wait_group(g)
         raw = [scores(hd) for hd in range(n_head)]
-        q_new = project(0, base)
+        q_new = project(0, g)
         probs = [softmax(raw[hd]) for hd in range(n_head)]
         qbuf[...] = q_new
-        k_new = project(1, base)
+        k_new = project(1, g)
         kbuf[...] = k_new
         for hd in range(n_head):
             mix(g - 1, hd, probs[hd])
-        v_new = project(2, base)
+        v_new = project(2, g)
         vbuf[...] = v_new
         a_copy(g - 1).start()
-        refill(g, base)
+        for j in range(6):
+            refill(g, j)
         return carry
 
     lax.fori_loop(1, n_grp, group, 0)
@@ -350,13 +396,16 @@
     def out_cols(n):
         return pl.ds(pl.multiple_of(core * half + n * gw, gw), gw)
 
+    def z_cols(n):
+        return pl.ds(pl.multiple_of(n * gw, gw), gw)
+
     def out_local(n):
         rows = pl.ds(pl.multiple_of(core * tok_dev, tok_dev), tok_dev)
-        return pltpu.make_async_copy(zbuf.at[n, rows], z_hbm.at[:, out_cols(n)], outl.at[n])
+        return pltpu.make_async_copy(xbuf.at[rows, z_cols(n)], z_hbm.at[:, out_cols(n)], outl.at[n])
 
     def out_remote(n):
         rows = pl.ds(pl.multiple_of((1 - core) * tok_dev, tok_dev), tok_dev)
-        return remote(zbuf.at[n, rows], z_hbm.at[:, out_cols(n)], outs.at[n], outr.at[n], {"ep": partner})
+        return remote(xbuf.at[rows, z_cols(n)], z_hbm.at[:, out_cols(n)], outs.at[n], outr.at[n], {"ep": partner})
 
     def out_group(n, carry):
         for kq in range(4):
@@ -367,22 +416,25 @@
             for gg in range(grp_per_slot):
                 term = mm(abuf[kq * grp_per_slot + gg], wbuf[slot, gg * gw:(gg + 1) * gw, :])
                 acc = term if acc is None else acc + term
-        resid = ybuf[core, :, pl.ds(pl.multiple_of(n * gw, gw), gw)].astype(F32)
-        zbuf[n] = (resid + acc.astype(BF16).astype(F32)).astype(BF16)
+        xbuf[:, z_cols(n)] = acc.astype(BF16)
         out_local(n).start()
         out_remote(n).start()
         return carry
 
     lax.fori_loop(0, n_out, out_group, 0)
 
+    for b in range(2 * n_out):
+        y_out(b).wait()
     own_copy.wait_send()
     for cp in meta_copies:
         cp.wait_send()
-    for s in range(2 * n_chunk):
-        pair_copy(s, chunk_row(s)).wait_send()
+    for s in range(2 * n_chunk - 2, 2 * n_chunk):
+        pair_copy(s).wait_send()
+    for f in range(n_chunk - 1):
+        y_copy(2 * f, 2).wait_send()
+    for k in (n_piece - 2, n_piece - 1):
+        y_copy(k, 1).wait_send()
     for k in range(n_piece):
-        y_copy(k).wait_send()
-        z_copy(k).wait_send()
         fwd_copy(k).wait_send()
     for g in range(n_grp):
         a_copy(g).wait_send()
@@ -406,37 +458,40 @@
         n_out = d_model // 2 // gw
         tok_chip = 2 * tok_dev
         half = d_model // 2
-        vmem = pl.BlockSpec(memory_space=pltpu.VMEM)
         anym = pl.BlockSpec(memory_space=pl.ANY)
         dma = pltpu.SemaphoreType.DMA
         n_chunk2 = 2 * tok_chip // ROWS
         n_piece = tok_chip // PIECE
-        out = pl.pallas_call(
+        proj, y_own = pl.pallas_call(
             functools.partial(stage_kernel, n_pp, gw, exp_rows, cap),
-            out_shape=jax.ShapeDtypeStruct((tok_dev, d_model), BF16),
-            in_specs=[vmem] * 5 + [anym] * 6,
-            out_specs=anym,
+            out_shape=[jax.ShapeDtypeStruct((tok_dev, d_model), BF16)] * 2,
+            in_specs=[anym] * 11,
+            out_specs=[anym] * 2,
             scratch_shapes=[
+                pltpu.VMEM((8, tok_dev), jnp.int32),
+                pltpu.VMEM((8, tok_dev), jnp.int32),
+                pltpu.VMEM((8, tok_dev), F32),
+                pltpu.VMEM((1, owner.shape[1]), jnp.int32),
+                pltpu.VMEM((1, d_model), F32),
+                dma((5,)), dma((8,)),
                 pltpu.VMEM((SLOTS, d_model // 2, gw), BF16),
-                pltpu.VMEM((2, 4 * tok_dev, half), F32),
                 pltpu.VMEM((4 * tok_dev, half), F32),
+                pltpu.VMEM((2, ROWS, half), F32),
+                pltpu.VMEM((2, ROWS, half), F32),
                 pltpu.VMEM((tok_chip, half), F32),
-                pltpu.VMEM((tok_chip, half), BF16),
-                pltpu.VMEM((2, tok_chip, half), BF16),
+                pltpu.VMEM((2 * n_out, tok_chip, gw), BF16),
                 pltpu.VMEM((tok_chip, d_model), BF16),
                 pltpu.VMEM((tok_chip, gw), BF16),
                 pltpu.VMEM((tok_chip, gw), BF16),
                 pltpu.VMEM((tok_chip, gw), BF16),
                 pltpu.VMEM((2 * n_grp, tok_chip, gw), BF16),
-                pltpu.VMEM((n_out, tok_chip, gw), BF16),
-                pltpu.VMEM((tok_dev, d_model), BF16),
                 pltpu.VMEM((3 * ROWS, exp_rows), BF16),
                 pltpu.VMEM((N_EP, 16, LANES), F32),
                 pltpu.VMEM((4 * SEQ, LANES), F32),
                 pltpu.VMEM((4 * SEQ, LANES), F32),
                 pltpu.VMEM((4 * tok_dev, LANES), F32),
                 pltpu.VMEM((4 * tok_dev, LANES), F32),
-                dma((SLOTS,)), dma((8,)), dma,
+                dma((SLOTS,)), dma((8,)), dma((8,)),
                 dma((3,)), dma((3,)), dma, dma,
                 dma((n_chunk2,)), dma((n_chunk2,)),
                 dma((n_piece,)), dma((n_piece,)),
@@ -449,6 +504,7 @@
                 collective_id=0, has_side_effects=True, vmem_limit_bytes=67043328),
         )(expert_id[0, 0].T, slot_id[0, 0].T, gate[0, 0].T, owner, norm_w, expert_out.reshape(exp_rows, d_model), resid.reshape(tok_dev, d_model),
           w_q[0], w_k[0], w_v[0], w_o[0])
+        out = (y_own.astype(F32) + proj.astype(F32)).astype(BF16)
         return out.reshape(1, 1, tok_dev, d_model)
 
     tok_spec = P(group_axes, None, 'ep', None)

time: 76 us -> 73.1 us (0.962)
  Pallas kernels: 73.8 us -> 70.9 us
  other arithmetic: 0 us -> 2.12 us
  local copies, waits for them, and re-layouts: 1.87 us -> 0 us
    pallas_call x1, Pallas kernels: 73.8 us -> 70.9 us  [device_step(): pl.pallas_call(functools.partial(stage_kernel, n_pp, gw, exp_rows, cap),...]
    reshape x0 -> x1, other arithmetic: none -> 2.12 us  [device_step(): return out.reshape(1, 1, tok_dev, d_model)]
    unnamed x1 -> x0, local copies, waits for them, and re-layouts: 1.87 us -> none
where the time goes in v4:
time: 73.1 us; the launch traced here: 73 us
  Pallas kernels  70.9 us (97%)
  other arithmetic  2.12 us (3%)
    pallas_call x1, Pallas kernels, device_step(): pl.pallas_call(functools.partial(stage_kernel, n_pp, gw, exp_rows, cap),...  70.9 us
    reshape x1, other arithmetic, device_step(): return out.reshape(1, 1, tok_dev, d_model)  2.12 us

profile of v4, /device:TPU:0, one launch (start us, length us, event | category | flops | bytes accessed | tf_op | source)
XLA Modules:
  0.0 73.0 jit_solution(9653060205066781643)
XLA Ops:
  0.0 70.9 %shard_map.109 = (bf16[64,4096]{1,0:T(8,128)(2,1)}, bf16[64,4096]{1,0:T(8,128)(2,1)}) custom-call(s32[8,64]{1,0:T(8,128)} %bitcast.19, s32[8,64]{1,0:T(8,128)} %bitcast.20, f32[8,64]{1,0:T(8,128)} %bitcast.21, s32[1,32]{1,0:T(1,128)} %own_hbm.1, f32[1,4096]{1,0:T(1,128)} %nw_hbm.1, bf16[1024,4096]{1,0:T(8,128)(2,1)} %bitcast.17, bf16[64,4096]{1,0:T(8,128)(2,1)} %bitcast.18, ...), custom_call_target="tpu_custom_call" | custom-call | tf_op jit(solution)/shard_map/pallas_call | solution.py:465
  70.9 2.1 %fusion = bf16[1,1,64,4096]{3,2,1,0:T(8,128)(2,1)} fusion(bf16[64,4096]{1,0:T(8,128)(2,1)} %get-tuple-element.8, bf16[64,4096]{1,0:T(8,128)(2,1)} %get-tuple-element.7), kind=kLoop, calls=%fused_computation.1 | loop fusion | flops 1048576 | bytes 1572864 | tf_op jit(solution)/shard_map/reshape | solution.py:508

commit v5 on v4

--- a/solution.py
+++ b/solution.py
@@ -41,11 +41,11 @@
 def stage_kernel(
     n_pp, gw, exp_rows, cap,
     eid_hbm, slot_hbm, gate_hbm, own_hbm, nw_hbm, o_hbm, h_hbm, wq_hbm, wk_hbm, wv_hbm, wo_hbm,
-    z_hbm, y_hbm,
-    eid_ref, slot_ref, gate_ref, own_ref, nw_ref, insem, youtsem,
-    wbuf, pkeep, pout, precv, yrecv, ybuf, xbuf, qbuf, kbuf, vbuf, abuf, gbuf, metas, owns, ownr, tok, mp,
+    z_ref,
+    eid_ref, slot_ref, gate_ref, own_ref, nw_ref, insem,
+    wbuf, pkeep, pout, precv, yrecv, ybuf, xbuf, qbuf, kbuf, vbuf, abuf, metas, owns, tok, mp,
     wsem, osem, hsem, msend, mrecv, osend, orecv, psend, prcv, ysend, yrcv, zsnd, zrcv, fsend, frcv, asend, arcv,
-    outl, outs, outr,
+    outs, outr,
 ):
     d_model = nw_hbm.shape[1]
     half = d_model // 2
@@ -124,7 +124,7 @@
     own_col = jnp.sum(jnp.where(diag, own_row, 0.0), axis=1, keepdims=True)
     owns[...] = jnp.broadcast_to(own_col, (n_seq, LANES))
     pl.semaphore_wait(barrier, 5)
-    own_copy = remote(owns, ownr, osend, orecv, {"pp": prv})
+    own_copy = remote(owns, mp.at[pl.ds(0, 4 * SEQ)], osend, orecv, {"pp": prv})
     own_copy.start()
     meta_copies = [
         remote(metas.at[me], metas.at[me], msend.at[off - 1], mrecv.at[off - 1], {"ep": lax.rem(me + off, N_EP)})
@@ -137,7 +137,7 @@
     own_copy.wait_recv()
     sub = lax.broadcasted_iota(jnp.int32, (SEQ, LANES), 0).astype(F32)
     for b in range(4 * SEQ):
-        row = jnp.broadcast_to(ownr[b:b + 1, :], (SEQ, LANES))
+        row = jnp.broadcast_to(mp[b:b + 1, :], (SEQ, LANES))
         tok[b * SEQ:(b + 1) * SEQ, :] = row * float(SEQ) + sub
     for cp in meta_copies:
         cp.wait_recv()
@@ -156,8 +156,7 @@
         h_copy(nb).wait()
 
     def pair_copy(s):
-        slot = lax.rem(s, 2)
-        return remote(pout.at[slot], precv.at[slot], psend.at[s], prcv.at[s], {"ep": partner})
+        return remote(pout, precv.at[lax.rem(s, 2)], psend.at[s], prcv.at[s], {"ep": partner})
 
     def y_copy(k, n):
         src = pl.ds(pl.multiple_of((1 - chip) * tok_chip + k * PIECE, PIECE), n * PIECE)
@@ -246,6 +245,9 @@
             xbuf[rows, cols] = (ybuf[b, rows, :].astype(F32) * inv * nw_ref[:, cols]).astype(BF16)
 
     z_lag, f_lag, first_z = 4, 6, 2
+
+    g_blk = core * n_grp + n_out
+    gcol = min(256, gw)
 
     def chunk(s, carry):
         row0 = chunk_row(s)
@@ -263,26 +265,29 @@
                 g0 = jnp.where(hit, here[:, 8 + j:9 + j], g0)
                 g1 = jnp.where(hit, here[:, 24 + j:25 + j], g1)
                 g2 = jnp.where(hit, here[:, 40 + j:41 + j], g2)
-            cols = slice(cb * 256, (cb + 1) * 256)
-            gbuf[0:ROWS, cols] = g0.astype(BF16)
-            gbuf[ROWS:2 * ROWS, cols] = g1.astype(BF16)
-            gbuf[2 * ROWS:3 * ROWS, cols] = g2.astype(BF16)
+            for part, val in enumerate((g0, g1, g2)):
+                for c0 in range(0, 256, gcol):
+                    at = cb * 256 + c0
+                    abuf[g_blk + at // gw, part * ROWS:(part + 1) * ROWS, at % gw:at % gw + gcol] = val[:, c0:c0 + gcol].astype(BF16)
         lane_h = lax.broadcasted_iota(jnp.int32, (ROWS, LANES), 1).astype(F32)
         is_mine = (tok[rows, :] - (me * tok_dev).astype(F32) == lane_h) & (lane_h < float(tok_dev))
         pick = jnp.where(is_mine, 1.0, 0.0).astype(BF16)[:, :tok_dev]
-        @pl.when(s >= 2)
-        def _():
-            pair_copy(s - 2).wait_send()
+        @pl.when(s >= 1)
+        def _():
+            pair_copy(s - 1).wait_send()
 
         for side in range(2):
             hh = (1 - core) if side == 0 else core
             for q in range(4):
                 o_cols = wbuf[o_slot + 2 * hh + q // 2, (q % 2) * exp_rows:(q % 2 + 1) * exp_rows, :]
                 h_cols = abuf[(1 - core) * n_grp + hh * n_out + q, 0:tok_dev, :]
-                p3 = mm(gbuf[...], o_cols)
+                p3 = None
+                for kb in range(exp_rows // gw):
+                    term = mm(abuf[g_blk + kb, 0:3 * ROWS, :], o_cols[kb * gw:(kb + 1) * gw, :])
+                    p3 = term if p3 is None else p3 + term
                 total = p3[0:ROWS] + p3[ROWS:2 * ROWS] + p3[2 * ROWS:3 * ROWS] + mm(pick, h_cols)
                 if side == 0:
-                    pout[lax.rem(s, 2), :, q * gw:(q + 1) * gw] = total
+                    pout[:, q * gw:(q + 1) * gw] = total
                 else:
                     pkeep[rows, q * gw:(q + 1) * gw] = total
             if side == 0:
@@ -353,12 +358,6 @@
         for j in range(6):
             qkv_copy(j // 2, j % 2, g, slot_of(g, j)).wait()
 
-    def y_out(b):
-        rows = pl.ds(pl.multiple_of(core * tok_dev, tok_dev), tok_dev)
-        return pltpu.make_async_copy(ybuf.at[b, rows], y_hbm.at[:, pl.ds(b * gw, gw)], youtsem.at[b])
-
-    for b in range(2 * n_out):
-        y_out(b).start()
     for k in range(n_piece):
         z_copy(k).wait_send()
     wait_group(0)
@@ -399,37 +398,44 @@
     def z_cols(n):
         return pl.ds(pl.multiple_of(n * gw, gw), gw)
 
-    def out_local(n):
-        rows = pl.ds(pl.multiple_of(core * tok_dev, tok_dev), tok_dev)
-        return pltpu.make_async_copy(xbuf.at[rows, z_cols(n)], z_hbm.at[:, out_cols(n)], outl.at[n])
-
     def out_remote(n):
         rows = pl.ds(pl.multiple_of((1 - core) * tok_dev, tok_dev), tok_dev)
-        return remote(xbuf.at[rows, z_cols(n)], z_hbm.at[:, out_cols(n)], outs.at[n], outr.at[n], {"ep": partner})
+        return remote(xbuf.at[rows, z_cols(n)], z_ref.at[:, out_cols(n)], outs.at[n], outr.at[n], {"ep": partner})
+
+    def out_part(n, kq):
+        slot = lax.rem(6 * n_grp + 4 * n + kq, SLOTS)
+        acc = None
+        for gg in range(grp_per_slot):
+            term = mm(abuf[kq * grp_per_slot + gg], wbuf[slot, gg * gw:(gg + 1) * gw, :])
+            acc = term if acc is None else acc + term
+        return acc
+
+    def out_done(n, acc):
+        resid = ybuf[core * n_out + n].astype(F32)
+        xbuf[:, z_cols(n)] = (resid + acc.astype(BF16).astype(F32)).astype(BF16)
+        out_remote(n).start()
+        mine = pl.ds(pl.multiple_of(core * tok_dev, tok_dev), tok_dev)
+        z_ref[:, out_cols(n)] = xbuf[mine, z_cols(n)]
 
     def out_group(n, carry):
         for kq in range(4):
             wo_copy(4 * n + kq).wait()
-        acc = None
-        for kq in range(4):
-            slot = lax.rem(6 * n_grp + 4 * n + kq, SLOTS)
-            for gg in range(grp_per_slot):
-                term = mm(abuf[kq * grp_per_slot + gg], wbuf[slot, gg * gw:(gg + 1) * gw, :])
-                acc = term if acc is None else acc + term
-        xbuf[:, z_cols(n)] = acc.astype(BF16)
-        out_local(n).start()
-        out_remote(n).start()
+        out_done(n, out_part(n, 0) + out_part(n, 1) + out_part(n, 2) + out_part(n, 3))
         return carry
 
-    lax.fori_loop(0, n_out, out_group, 0)
-
-    for b in range(2 * n_out):
-        y_out(b).wait()
+    lax.fori_loop(0, n_out - 1, out_group, 0)
+    end = n_out - 1
+    total = None
+    for kq in range(4):
+        wo_copy(4 * end + kq).wait()
+        part = out_part(end, kq)
+        total = part if total is None else total + part
+    out_done(end, total)
+
     own_copy.wait_send()
     for cp in meta_copies:
         cp.wait_send()
-    for s in range(2 * n_chunk - 2, 2 * n_chunk):
-        pair_copy(s).wait_send()
+    pair_copy(2 * n_chunk - 1).wait_send()
     for f in range(n_chunk - 1):
         y_copy(2 * f, 2).wait_send()
     for k in (n_piece - 2, n_piece - 1):
@@ -439,7 +445,6 @@
     for g in range(n_grp):
         a_copy(g).wait_send()
     for n in range(n_out):
-        out_local(n).wait()
         out_remote(n).wait()
 
 
@@ -462,21 +467,21 @@
         dma = pltpu.SemaphoreType.DMA
         n_chunk2 = 2 * tok_chip // ROWS
         n_piece = tok_chip // PIECE
-        proj, y_own = pl.pallas_call(
+        out = pl.pallas_call(
             functools.partial(stage_kernel, n_pp, gw, exp_rows, cap),
-            out_shape=[jax.ShapeDtypeStruct((tok_dev, d_model), BF16)] * 2,
+            out_shape=pltpu.VMEM((tok_dev, d_model), BF16),
             in_specs=[anym] * 11,
-            out_specs=[anym] * 2,
+            out_specs=pl.BlockSpec(memory_space=pltpu.VMEM),
             scratch_shapes=[
                 pltpu.VMEM((8, tok_dev), jnp.int32),
                 pltpu.VMEM((8, tok_dev), jnp.int32),
                 pltpu.VMEM((8, tok_dev), F32),
                 pltpu.VMEM((1, owner.shape[1]), jnp.int32),
                 pltpu.VMEM((1, d_model), F32),
-                dma((5,)), dma((8,)),
+                dma((5,)),
                 pltpu.VMEM((SLOTS, d_model // 2, gw), BF16),
                 pltpu.VMEM((4 * tok_dev, half), F32),
-                pltpu.VMEM((2, ROWS, half), F32),
+                pltpu.VMEM((ROWS, half), F32),
                 pltpu.VMEM((2, ROWS, half), F32),
                 pltpu.VMEM((tok_chip, half), F32),
                 pltpu.VMEM((2 * n_out, tok_chip, gw), BF16),
@@ -485,9 +490,7 @@
                 pltpu.VMEM((tok_chip, gw), BF16),
                 pltpu.VMEM((tok_chip, gw), BF16),
                 pltpu.VMEM((2 * n_grp, tok_chip, gw), BF16),
-                pltpu.VMEM((3 * ROWS, exp_rows), BF16),
                 pltpu.VMEM((N_EP, 16, LANES), F32),
-                pltpu.VMEM((4 * SEQ, LANES), F32),
                 pltpu.VMEM((4 * SEQ, LANES), F32),
                 pltpu.VMEM((4 * tok_dev, LANES), F32),
                 pltpu.VMEM((4 * tok_dev, LANES), F32),
@@ -498,13 +501,12 @@
                 dma((n_piece,)), dma((n_piece,)),
                 dma((n_piece,)), dma((n_piece,)),
                 dma((n_grp,)), dma((n_grp,)),
-                dma((n_out,)), dma((n_out,)), dma((n_out,)),
+                dma((n_out,)), dma((n_out,)),
             ],
             compiler_params=pltpu.CompilerParams(
-                collective_id=0, has_side_effects=True, vmem_limit_bytes=67043328),
+                collective_id=0, has_side_effects=True, vmem_limit_bytes=66519040),
         )(expert_id[0, 0].T, slot_id[0, 0].T, gate[0, 0].T, owner, norm_w, expert_out.reshape(exp_rows, d_model), resid.reshape(tok_dev, d_model),
           w_q[0], w_k[0], w_v[0], w_o[0])
-        out = (y_own.astype(F32) + proj.astype(F32)).astype(BF16)
         return out.reshape(1, 1, tok_dev, d_model)
 
     tok_spec = P(group_axes, None, 'ep', None)

time: 73.1 us -> 70.9 us (0.970)
  other arithmetic: 2.12 us -> 0 us
  Pallas kernels: 70.9 us -> 69.9 us
  local copies, waits for them, and re-layouts: 0 us -> 0.8 us
    reshape x1 -> x0, other arithmetic: 2.12 us -> none  [device_step(): return out.reshape(1, 1, tok_dev, d_model)]
    pallas_call x1, Pallas kernels: 70.9 us -> 69.9 us  [device_step(): pl.pallas_call(functools.partial(stage_kernel, n_pp, gw, exp_rows, cap),...]
    unnamed x0 -> x1, local copies, waits for them, and re-layouts: none -> 0.8 us
where the time goes in v5:
time: 70.9 us; the launch traced here: 70.7 us
  Pallas kernels  69.9 us (99%)
  local copies, waits for them, and re-layouts  0.8 us (1%)
    pallas_call x1, Pallas kernels, device_step(): pl.pallas_call(functools.partial(stage_kernel, n_pp, gw, exp_rows, cap),...  69.9 us

profile of v5, /device:TPU:0, one launch (start us, length us, event | category | flops | bytes accessed | tf_op | source)
XLA Modules:
  0.0 70.7 jit_solution(12397152167124932431)
XLA Ops:
  0.0 69.9 %shard_map.109 = bf16[64,4096]{1,0:T(8,128)(2,1)S(1)} custom-call(s32[8,64]{1,0:T(8,128)} %bitcast.19, s32[8,64]{1,0:T(8,128)} %bitcast.20, f32[8,64]{1,0:T(8,128)} %bitcast.21, s32[1,32]{1,0:T(1,128)} %own_hbm.1, f32[1,4096]{1,0:T(1,128)} %nw_hbm.1, bf16[1024,4096]{1,0:T(8,128)(2,1)} %bitcast.17, bf16[64,4096]{1,0:T(8,128)(2,1)} %bitcast.18, ...), custom_call_target="tpu_custom_call" | custom-call | tf_op jit(solution)/shard_map/pallas_call | solution.py:470
  69.9 0.8 %copy.13 = bf16[1,1,64,4096]{3,2,1,0:T(8,128)(2,1)} copy(bf16[1,1,64,4096]{3,2,1,0:T(8,128)(2,1)S(1)} %bitcast.16) | data formatting | bytes 1048576

commit v6 on v5

--- a/solution.py
+++ b/solution.py
@@ -163,6 +163,13 @@
         dst = pl.ds(pl.multiple_of(k * PIECE, PIECE), n * PIECE)
         return remote(pkeep.at[src], yrecv.at[dst], ysend.at[k], yrcv.at[k], {"ep": across})
 
+    def y_tail(h):
+        src = pl.ds(pl.multiple_of((1 - chip) * tok_chip + (n_piece - 1) * PIECE, PIECE), PIECE)
+        dst = pl.ds((n_piece - 1) * PIECE, PIECE)
+        cols = pl.ds(h * (half // 2), half // 2)
+        at = n_piece - 1 + h
+        return remote(pkeep.at[src, cols], yrecv.at[dst, cols], ysend.at[at], yrcv.at[at], {"ep": across})
+
     def chunk_of(s):
         end = 2 * n_chunk - 1
         far = lax.rem(s, 2) + (end - s) // end - s // end
@@ -188,7 +195,8 @@
         @pl.when(far * (idx // (n_chunk - 1)) > 0)
         def _():
             y_copy(n_piece - 2, 1).start()
-            y_copy(n_piece - 1, 1).start()
+            y_tail(0).start()
+            y_tail(1).start()
 
     def prefetch(t):
         g, kh = t // 2, lax.rem(t, 2)
@@ -210,25 +218,44 @@
             abuf.at[pl.ds(core * n_grp, n_out), piece(k)], ybuf.at[pl.ds(core * n_out, n_out), piece(k)],
             zsnd.at[k], zrcv.at[k], {"pp": nxt})
 
+    def z_tail(h):
+        at, n = n_piece - 1 + h, n_out // 2
+        return remote(
+            abuf.at[pl.ds(core * n_grp + h * n, n), piece(n_piece - 1)],
+            ybuf.at[pl.ds(core * n_out + h * n, n), piece(n_piece - 1)], zsnd.at[at], zrcv.at[at], {"pp": nxt})
+
     def fwd_copy(k):
         half_rows = ybuf.at[pl.ds(core * n_out, n_out), piece(k)]
         return remote(half_rows, half_rows, fsend.at[k], frcv.at[k], {"ep": partner})
 
+    def round_rows(k, blocks):
+        near = pl.ds(pl.multiple_of(chip * tok_chip + k * PIECE, PIECE), PIECE)
+        for b in blocks:
+            cols = slice(b * gw, (b + 1) * gw)
+            abuf[core * n_grp + b, piece(k), :] = (pkeep[near, cols] + yrecv[piece(k), cols]).astype(BF16)
+
     def step_y(k):
+        if isinstance(k, int) and k == n_piece - 1:
+            for h in range(2):
+                y_tail(h).wait_recv()
+                round_rows(k, range(h * n_out // 2, (h + 1) * n_out // 2))
+                z_tail(h).start()
+            return
         if isinstance(k, int) and k >= n_piece - 2:
             y_copy(k, 1).wait_recv()
         else:
             @pl.when(lax.rem(k, 2) == 0)
             def _():
                 y_copy(k, 2).wait_recv()
-        near = pl.ds(pl.multiple_of(chip * tok_chip + k * PIECE, PIECE), PIECE)
-        for b in range(n_out):
-            cols = slice(b * gw, (b + 1) * gw)
-            abuf[core * n_grp + b, piece(k), :] = (pkeep[near, cols] + yrecv[piece(k), cols]).astype(BF16)
+        round_rows(k, range(n_out))
         z_copy(k).start()
 
     def step_z(k):
-        z_copy(k).wait_recv()
+        if isinstance(k, int) and k == n_piece - 1:
+            z_tail(0).wait_recv()
+            z_tail(1).wait_recv()
+        else:
+            z_copy(k).wait_recv()
         fwd_copy(k).start()
 
     def step_norm(k):
@@ -358,8 +385,10 @@
         for j in range(6):
             qkv_copy(j // 2, j % 2, g, slot_of(g, j)).wait()
 
-    for k in range(n_piece):
+    for k in range(n_piece - 1):
         z_copy(k).wait_send()
+    for h in range(2):
+        z_tail(h).wait_send()
     wait_group(0)
     for m, buf in enumerate((qbuf, kbuf, vbuf)):
         buf[...] = project(m, 0)
@@ -438,8 +467,9 @@
     pair_copy(2 * n_chunk - 1).wait_send()
     for f in range(n_chunk - 1):
         y_copy(2 * f, 2).wait_send()
-    for k in (n_piece - 2, n_piece - 1):
-        y_copy(k, 1).wait_send()
+    y_copy(n_piece - 2, 1).wait_send()
+    for h in range(2):
+        y_tail(h).wait_send()
     for k in range(n_piece):
         fwd_copy(k).wait_send()
     for g in range(n_grp):
@@ -497,8 +527,8 @@
                 dma((SLOTS,)), dma((8,)), dma((8,)),
                 dma((3,)), dma((3,)), dma, dma,
                 dma((n_chunk2,)), dma((n_chunk2,)),
-                dma((n_piece,)), dma((n_piece,)),
-                dma((n_piece,)), dma((n_piece,)),
+                dma((n_piece + 1,)), dma((n_piece + 1,)),
+                dma((n_piece + 1,)), dma((n_piece + 1,)),
                 dma((n_piece,)), dma((n_piece,)),
                 dma((n_grp,)), dma((n_grp,)),
                 dma((n_out,)), dma((n_out,)),

time: 70.9 us -> 70.6 us (level)
  no operation moved by 1% of the time
where the time goes in v6:
time: 70.6 us; the launch traced here: 70.4 us
  Pallas kernels  69.6 us (99%)
  local copies, waits for them, and re-layouts  0.8 us (1%)
    pallas_call x1, Pallas kernels, device_step(): pl.pallas_call(functools.partial(stage_kernel, n_pp, gw, exp_rows, cap),...  69.6 us

profile of v6, /device:TPU:0, one launch (start us, length us, event | category | flops | bytes accessed | tf_op | source)
XLA Modules:
  0.0 70.4 jit_solution(6548035201442597105)
XLA Ops:
  0.0 69.6 %shard_map.109 = bf16[64,4096]{1,0:T(8,128)(2,1)S(1)} custom-call(s32[8,64]{1,0:T(8,128)} %bitcast.19, s32[8,64]{1,0:T(8,128)} %bitcast.20, f32[8,64]{1,0:T(8,128)} %bitcast.21, s32[1,32]{1,0:T(1,128)} %own_hbm.1, f32[1,4096]{1,0:T(1,128)} %nw_hbm.1, bf16[1024,4096]{1,0:T(8,128)(2,1)} %bitcast.17, bf16[64,4096]{1,0:T(8,128)(2,1)} %bitcast.18, ...), custom_call_target="tpu_custom_call" | custom-call | tf_op jit(solution)/shard_map/pallas_call | solution.py:500
  69.6 0.8 %copy.13 = bf16[1,1,64,4096]{3,2,1,0:T(8,128)(2,1)} copy(bf16[1,1,64,4096]{3,2,1,0:T(8,128)(2,1)S(1)} %bitcast.16) | data formatting | bytes 1048576
